TPU v7x, 32 devices: a whole 2x2x4 slice. The times are simulated.
32 devices in a mesh: member: 8 (over y, x, core), region: 4 (over z).
Axes of the slice: x: 2, y: 2, z: 4, core: 2. Of those that a mesh axis runs over, the one named last changes fastest.
Arguments:
- prior_sample_matrix: float32 [128, 65536], P(('member', 'region')), may hold values from -18 to 18
- obs_values: float32 [1024], replicated, may hold values from -18 to 18
- obs_var: float32 [1024], replicated, may hold values from 0.5 to 4
- measured_indexes: int32 [1024], replicated, may hold values from 0 to 65535
- neighbours: int32 [128, 128], replicated, may hold values from 0 to 1023, as said below
- perturbation: float32 [128, 1024], P(('member', 'region')), may hold values from -6 to 6
- counts: int32 [32], replicated, may hold values from 1 to 8, as said below
Outputs:
- owned: float32 [256, 65536], P(('member', 'region'))
Inputs may be any that keep to these rules, and one draw needn't show every extreme that they name: `neighbours`: each row lists 128 different observations. The counts sum to 128; some device owns exactly 8; the exclusive prefix sum of counts at device d differs from d * 4 by at most 2.
All inputs are finite; a program needn't handle non-finite values.
Results may differ from a plain program's by a relative error of at most 0.0003.
Values sent between devices are 32-bit elements; how exact they have to be, the bound alone decides.
No kernel may reach another device: no remote copies, remote signals or barrier semaphores. Data moves between devices by JAX's collectives and lax.ppermute only.
A program may use at most 128 MiB of HBM per device.

v0:
```python
import functools

import jax
import jax.numpy as jnp
from jax import lax
from jax.experimental import pallas as pl
from jax.experimental.pallas import tpu as pltpu
from jax.sharding import PartitionSpec as P


PREDICT_SUBTICKS = 24
CAP = 8
LSCALE = 2048
FORCING = 8.0
TIME_STEP = 0.01
HIGH = lax.Precision.HIGHEST
AXES = ("member", "region")
LANES = 128
VMEM_PIECES = 1 << 20
ROWS = 8


def lanes_iota():
    return lax.broadcasted_iota(jnp.int32, (ROWS, LANES), 1)


def rows_iota():
    return lax.broadcasted_iota(jnp.int32, (ROWS, LANES), 0)


def forecast_kernel(places_ref, noise_ref, x_ref, state_ref, mine_ref, tile_ref, table_ref, scalar_ref, table_sem, *, members):
    height = x_ref.shape[0]
    blocks = places_ref.shape[0]
    tiles = height // LANES
    halves = tiles // ROWS
    tile_pitch = LANES + ROWS
    cell_pitch = tiles + ROWS
    parts = ROWS // members
    lane = lanes_iota()
    row = rows_iota()

    def group(cell):
        return [state_ref[cell * tiles + half * ROWS : cell * tiles + (half + 1) * ROWS, :] for half in range(halves)]

    for tile in range(tiles):
        tile_ref[tile * tile_pitch : tile * tile_pitch + LANES, :] = (x_ref[tile * LANES : (tile + 1) * LANES, :] * TIME_STEP).T
    for cell in range(LANES):
        for half in range(halves):
            begin = cell * tiles + half * ROWS
            state_ref[begin : begin + ROWS, :] = tile_ref[pl.ds(half * ROWS * tile_pitch + cell, ROWS, stride=tile_pitch), :]

    places = places_ref[...]
    column = lax.broadcasted_iota(jnp.int32, places.shape, 1)
    table_ref[:blocks, :] = (places // (LANES * parts)) * ROWS
    table_ref[blocks:, :] = (column - places) & (LANES - 1)
    table_copy = pltpu.make_async_copy(table_ref, scalar_ref, table_sem)
    table_copy.start()

    def next_run(values):
        turned = [pltpu.roll(value, LANES - members, axis=1) for value in values]
        down = [pltpu.roll(value, ROWS - 1, axis=0) for value in turned]
        carried = [jnp.where(row == ROWS - 1, down[(half + 1) % halves], down[half]) for half in range(halves)]
        return [jnp.where(lane >= LANES - members, carry, value) for carry, value in zip(carried, turned, strict=True)]

    def previous_run(values):
        turned = [pltpu.roll(value, members, axis=1) for value in values]
        up = [pltpu.roll(value, 1, axis=0) for value in turned]
        carried = [jnp.where(row == 0, up[half - 1], up[half]) for half in range(halves)]
        return [jnp.where(lane < members, carry, value) for carry, value in zip(carried, turned, strict=True)]

    def advance(left_two, left, current, right):
        return [
            (c * (1.0 - TIME_STEP) + FORCING * TIME_STEP * TIME_STEP) + (d - a) * b
            for a, b, c, d in zip(left_two, left, current, right, strict=True)
        ]

    def store(cell, values):
        for half in range(halves):
            begin = cell * tiles + half * ROWS
            state_ref[begin : begin + ROWS, :] = values[half]

    def substep(_, carry):
        before_two = previous_run(group(LANES - 2))
        before = previous_run(group(LANES - 1))
        first = [group(cell) for cell in range(3)]
        beyond = next_run(first[0])
        window = list(first)
        for cell in range(2, LANES - 1):
            right = group(cell + 1)
            store(cell, advance(*window, right))
            window = window[1:] + [right]
        store(LANES - 1, advance(*window, beyond))
        store(0, advance(before_two, before, first[0], first[1]))
        store(1, advance(before, first[0], first[1], first[2]))
        return carry

    lax.fori_loop(0, PREDICT_SUBTICKS, substep, 0)

    for cell in range(LANES):
        for half in range(halves):
            begin = cell * cell_pitch + half * ROWS
            tile_ref[begin : begin + ROWS, :] = group(cell)[half]
    for tile in range(tiles):
        state_ref[tile * LANES : (tile + 1) * LANES, :] = tile_ref[pl.ds(tile, LANES, stride=cell_pitch), :].T * (1.0 / TIME_STEP)
    table_copy.wait()

    def gather(block, carry):
        picked = [jnp.zeros((ROWS, LANES), jnp.float32) for _ in range(4)]
        for number in range(LANES):
            begin = pl.multiple_of(scalar_ref[block, number], ROWS)
            turned = pltpu.roll(state_ref[pl.ds(begin, ROWS), :], scalar_ref[blocks + block, number], axis=1)
            picked[number % 4] = jnp.where(lane == number, turned, picked[number % 4])
        both = picked[0]
        for number in range(1, 4):
            both = jnp.where(lane % 4 == number, picked[number], both)
        part_of = (places_ref[pl.ds(block, 1), :] // LANES) % parts
        chosen = both
        for part in range(1, parts):
            chosen = jnp.where(part_of == part, pltpu.roll(both, ROWS - part * members, axis=0), chosen)
        mine_ref[pl.ds(block * members, members), :] = chosen[:members]
        return carry

    lax.fori_loop(0, blocks, gather, 0)
    for block in range(blocks):
        begin = (blocks + block) * members
        mine_ref[begin : begin + members, :] = noise_ref[:, block * LANES : (block + 1) * LANES]


def dot(a, b, contract, precision=HIGH):
    return lax.dot_general(a, b, (contract, ((), ())), precision=precision, preferred_element_type=jnp.float32)


def split_three(value):
    high = value.astype(jnp.bfloat16)
    rest = value - high.astype(jnp.float32)
    middle = rest.astype(jnp.bfloat16)
    return high, middle, (rest - middle.astype(jnp.float32)).astype(jnp.bfloat16)


def invert_all(matrix_ref):
    regions, size, _ = matrix_ref.shape
    lane = lanes_iota()
    row = rows_iota()

    def panel(number, carry):
        base = number * ROWS
        start = pl.multiple_of(base, ROWS)
        offset = lane - base
        inside = (offset >= 0) & (offset < ROWS)
        unit = jnp.where(offset == row, 1.0, 0.0)
        blocks = [matrix_ref[region, pl.ds(start, ROWS), :] for region in range(regions)]
        columns = []
        for k in range(ROWS):
            index = jnp.full((ROWS, LANES), base + k, jnp.int32)
            columns.append([jnp.take_along_axis(block, index, axis=1) for block in blocks])
        lefts = []
        for block in blocks:
            signed = jnp.where(inside, 0.0, jnp.where(offset < 0, block, -block))
            high, middle, low = split_three(signed)
            lefts.append(jnp.concatenate([high, high, middle, high, low, middle], axis=0))
        blocks = [jnp.where(inside, unit, block) for block in blocks]
        for j in range(ROWS):
            here = row == j
            for region in range(regions):
                pivot = columns[j][region]
                inverse = 1.0 / pivot[j : j + 1, :]
                scaled = blocks[region][j : j + 1, :] * inverse
                blocks[region] = jnp.where(here, scaled, blocks[region] - pivot * scaled)
                for k in range(j + 1, ROWS):
                    scaled = columns[k][region][j : j + 1, :] * inverse
                    columns[k][region] = jnp.where(here, scaled, columns[k][region] - pivot * scaled)
        for region in range(regions):
            high, middle, low = split_three(blocks[region])
            right = jnp.concatenate([high, middle, high, low, high, middle], axis=0)
            update = dot(lefts[region], right, ((0,), (0,)), lax.Precision.DEFAULT)
            for i in range(size // ROWS):
                rows = slice(i * ROWS, (i + 1) * ROWS)
                matrix_ref[region, rows, :] = jnp.where(inside, 0.0, matrix_ref[region, rows, :]) + update[rows]
            matrix_ref[region, pl.ds(start, ROWS), :] = blocks[region]
        return carry

    lax.fori_loop(0, size // ROWS, panel, 0)


def split_two(value):
    high = value.astype(jnp.bfloat16)
    return high, (value - high.astype(jnp.float32)).astype(jnp.bfloat16)


def dot_split(a, b, contract):
    a_high, a_low = split_two(a)
    b_high, b_low = split_two(b)
    low = dot(a_high, b_low, contract, lax.Precision.DEFAULT) + dot(a_low, b_high, contract, lax.Precision.DEFAULT)
    return dot(a_high, b_high, contract, lax.Precision.DEFAULT) + low


def prepare_kernel(zone_ref, neighbours_ref, variance_ref, places_ref, pick_ref, errors_ref, *, cells, zone_cells):
    regions, observations, size = pick_ref.shape
    ids = lax.broadcasted_iota(jnp.int32, (observations, size), 0)
    rows = jnp.concatenate([variance_ref[...], places_ref[...].astype(jnp.float32), jnp.zeros((ROWS - 2, observations), jnp.float32)])
    pieces = jnp.concatenate(split_three(rows))
    for region in range(regions):
        zone = zone_ref[0] + region
        pick = jnp.where(ids == neighbours_ref[pl.ds(zone, 1), :], 1.0, 0.0).astype(jnp.bfloat16)
        pick_ref[region, :, :] = pick
        picked = dot(pieces, pick, ((1,), (0,)), lax.Precision.DEFAULT)
        picked = picked[:ROWS] + picked[ROWS : 2 * ROWS] + picked[2 * ROWS :]
        centre = (zone * zone_cells + zone_cells // 2).astype(jnp.float32)
        gap = jnp.abs(picked[1:2] - centre)
        scaled = jnp.minimum(gap, cells - gap) / float(LSCALE)
        errors_ref[region : region + 1, :] = picked[0:1] * (1.0 + scaled * scaled)


def solve_kernel(me_ref, pick_ref, errors_ref, values_ref, variance_ref, *refs, masks):
    *blocks_refs, transform_ref, stack_ref, pieces_ref, matrix_ref = refs
    regions, total, _ = transform_ref.shape
    observations = values_ref.shape[1]
    blocks = observations // LANES
    members = blocks_refs[0].shape[1] // (2 * blocks)
    size = pick_ref.shape[2]
    for block in range(blocks):
        lanes = slice(block * LANES, (block + 1) * LANES)
        values = values_ref[:, lanes]
        spread = jnp.sqrt(variance_ref[:, lanes])
        for blocks_ref, mask in zip(blocks_refs, masks, strict=True):
            for number, bits in enumerate(mask):
                source = pl.multiple_of(lax.bitwise_xor(me_ref[0], bits) * members, members)
                equivalents = blocks_ref[number, block * members : (block + 1) * members, :]
                noise = blocks_ref[number, (blocks + block) * members : (blocks + block + 1) * members, :]
                stack_ref[block, pl.ds(source, members), :] = equivalents
                stack_ref[block, pl.ds(total + source, members), :] = values + spread * noise - equivalents
        for number, piece in enumerate(split_two(stack_ref[block])):
            pieces_ref[number * 2 * total : (number + 1) * 2 * total, lanes] = piece
    diagonal = lax.broadcasted_iota(jnp.int32, (size, size), 0) == lax.broadcasted_iota(jnp.int32, (size, size), 1)
    anomalies, innovations = [], []
    for region in range(regions):
        picked = dot(pieces_ref[...], pick_ref[region], ((1,), (0,)), lax.Precision.DEFAULT)
        picked = picked[: 2 * total] + picked[2 * total :]
        equivalents = picked[:total]
        innovations.append(picked[total:])
        anomaly = equivalents - jnp.sum(equivalents, axis=0, keepdims=True) * (1.0 / total)
        anomalies.append(anomaly)
        covariance = dot(anomaly, anomaly, ((0,), (0,))) * (1.0 / (total - 1))
        matrix_ref[region, :, :] = jnp.where(diagonal, covariance + errors_ref[region : region + 1, :], covariance)
    invert_all(matrix_ref)
    for region in range(regions):
        weights = dot_split(innovations[region], matrix_ref[region], ((1,), (0,)))
        transform_ref[region, :, :] = dot_split(weights, anomalies[region], ((1,), (1,))) * (1.0 / (total - 1))


def apply_kernel(counts_ref, transform_ref, cells_ref, owned_ref, block_ref, result_ref):
    sources, height, _ = cells_ref.shape
    regions, total, _ = transform_ref.shape
    members = total // sources
    tiles = height // members
    for tile in range(tiles):
        lanes = slice(tile * LANES, (tile + 1) * LANES)
        for source in range(sources):
            block_ref[source * members : (source + 1) * members, lanes] = cells_ref[source, tile * members : (tile + 1) * members, :]
    wide = tiles // regions
    for region in range(regions):
        block = block_ref[:, region * wide * LANES : (region + 1) * wide * LANES]
        anomalies = block - jnp.sum(block, axis=0, keepdims=True) * (1.0 / total)
        analysed = block + dot_split(transform_ref[region], anomalies, ((1,), (0,)))
        for place in range(wide):
            result_ref[region * wide + place, :total, :] = analysed[:, place * LANES : (place + 1) * LANES]
    for tile in range(tiles):
        result_ref[tile, total:, :] = jnp.zeros((ROWS, LANES), jnp.float32)

    def window(destination, offset):
        for tile in range(tiles):
            owned_ref[destination, tile * ROWS : (tile + 1) * ROWS, :] = result_ref[tile, pl.ds(offset, CAP), :]
        return offset + counts_ref[destination]

    lax.fori_loop(0, sources, window, jnp.int32(0))


def advance_kernel(count_ref, rows_ref, out_ref):
    sources, height, _ = rows_ref.shape
    tiles = height // ROWS
    here = out_ref.shape[1] // LANES // tiles
    lane = lanes_iota()
    occupied = rows_iota() < count_ref[0]
    start = pl.program_id(0) * here

    def load(source, tile):
        return rows_ref[source, tile * ROWS : (tile + 1) * ROWS, :]

    before = load(lax.rem(start + sources - 1, sources), tiles - 1)
    before_one = pltpu.roll(before, 1, axis=1)
    before_two = pltpu.roll(before, 2, axis=1)
    current = load(start, 0)
    current_up = pltpu.roll(current, LANES - 1, axis=1)
    for number in range(here * tiles):
        source, tile = divmod(number + 1, tiles)
        after = load(start + source if source < here else lax.rem(start + here, sources), tile)
        after_up = pltpu.roll(after, LANES - 1, axis=1)
        one = pltpu.roll(current, 1, axis=1)
        two = pltpu.roll(current, 2, axis=1)
        left = jnp.where(lane == 0, before_one, one)
        left_two = jnp.where(lane < 2, before_two, two)
        right = jnp.where(lane == LANES - 1, after_up, current_up)
        stepped = current + TIME_STEP * ((right - left_two) * left - current + FORCING)
        out_ref[:, number * LANES : (number + 1) * LANES] = jnp.where(occupied, stepped, 0.0)
        before_one, before_two = one, two
        current, current_up = after, after_up


def whole(space=pltpu.VMEM):
    return pl.BlockSpec(memory_space=space)


def in_vmem(value):
    return pltpu.with_memory_space_constraint(value, pltpu.VMEM)


def per_device(prior_sample_matrix, obs_values, obs_var, measured_indexes, neighbours, perturbation, counts):
    devices = lax.axis_size(AXES)
    depth = lax.axis_size("region")
    device_index = lax.axis_index(AXES)
    me = device_index.reshape(1)
    members, cells = prior_sample_matrix.shape
    total = members * devices
    observations = obs_values.shape[0]
    zones, local = neighbours.shape
    regions = zones // devices
    zone_cells = cells // zones
    blocks = observations // LANES
    share_tiles = cells // devices // LANES
    values = obs_values.reshape(1, observations)
    variance = obs_var.reshape(1, observations)

    def swap(value, bits):
        return lax.ppermute(value, AXES, [(device, device ^ bits) for device in range(devices)])

    exchange = functools.partial(lax.all_to_all, axis_name=AXES, split_axis=0, concat_axis=0, tiled=True)

    pick, errors = pl.pallas_call(
        functools.partial(prepare_kernel, cells=float(cells), zone_cells=zone_cells),
        out_shape=(
            jax.ShapeDtypeStruct((regions, observations, local), jnp.bfloat16),
            jax.ShapeDtypeStruct((regions, local), jnp.float32),
        ),
        in_specs=[whole(pltpu.SMEM), whole(), whole(), whole()],
        out_specs=(whole(),) * 2,
        name="prepare",
    )(me * regions, neighbours, variance, measured_indexes.reshape(1, observations))

    runs = prior_sample_matrix.reshape(members, cells // LANES, LANES).transpose(1, 0, 2).reshape(-1, LANES)
    height = runs.shape[0]
    tiles = height // LANES
    state, mine = pl.pallas_call(
        functools.partial(forecast_kernel, members=members),
        out_shape=(
            jax.ShapeDtypeStruct((height, LANES), jnp.float32),
            jax.ShapeDtypeStruct((2 * blocks * members, LANES), jnp.float32),
        ),
        in_specs=[whole()] * 3,
        out_specs=(whole(),) * 2,
        scratch_shapes=[
            pltpu.VMEM((max(tiles * (LANES + ROWS), LANES * (tiles + ROWS)), LANES), jnp.float32),
            pltpu.VMEM((2 * blocks, LANES), jnp.int32),
            pltpu.SMEM((2 * blocks, LANES), jnp.int32),
            pltpu.SemaphoreType.DMA,
        ],
        name="forecast",
    )(measured_indexes.reshape(blocks, LANES), perturbation, runs)

    near = jnp.concatenate([mine[None]] + [swap(mine[None], bits) for bits in range(1, depth)])
    near_mask = list(range(depth))
    far_masks = [[chip * 2 * depth + bits for bits in near_mask] for chip in range(1, devices // (2 * depth))]
    far = []
    for mask in far_masks:
        far.append(swap(near, mask[0]))
    state, near = lax.optimization_barrier((state, near))
    own_cells = exchange(state.reshape(devices, height // devices, LANES))
    partner = swap(near, depth)
    partners = swap(jnp.concatenate(far), depth)
    pieces = [near, partner, *far, partners]
    masks = [near_mask, [depth ^ bits for bits in near_mask], *far_masks, [depth ^ bits for mask in far_masks for bits in mask]]

    place = in_vmem if sum(piece.size for piece in pieces) * 4 <= VMEM_PIECES else lambda value: value
    transform = pl.pallas_call(
        functools.partial(solve_kernel, masks=masks),
        out_shape=jax.ShapeDtypeStruct((regions, total, total), jnp.float32),
        in_specs=[whole(pltpu.SMEM)] + [whole()] * (4 + len(pieces)),
        out_specs=whole(),
        scratch_shapes=[
            pltpu.VMEM((blocks, 2 * total, LANES), jnp.float32),
            pltpu.VMEM((4 * total, observations), jnp.bfloat16),
            pltpu.VMEM((regions, local, local), jnp.float32),
        ],
        name="solve",
    )(me, pick, errors, values, variance, *map(place, pieces))

    outgoing = pl.pallas_call(
        apply_kernel,
        out_shape=jax.ShapeDtypeStruct((devices, share_tiles * CAP, LANES), jnp.float32),
        in_specs=[whole(pltpu.SMEM), whole(), whole()],
        out_specs=whole(),
        scratch_shapes=[
            pltpu.VMEM((total, share_tiles * LANES), jnp.float32),
            pltpu.VMEM((share_tiles, total + ROWS, LANES), jnp.float32),
        ],
        name="analyse",
    )(counts, transform, in_vmem(own_cells))
    owned = exchange(outgoing)

    steps = 4
    return pl.pallas_call(
        advance_kernel,
        grid=(steps,),
        out_shape=jax.ShapeDtypeStruct((CAP, cells), jnp.float32),
        in_specs=[whole(pltpu.SMEM), whole()],
        out_specs=pl.BlockSpec((CAP, cells // steps), lambda i: (0, i)),
        name="advance",
    )(lax.dynamic_slice_in_dim(counts, device_index, 1, 0), in_vmem(owned))


def solution(mesh):
    rows = P(AXES, None)
    return jax.shard_map(
        per_device, mesh=mesh, in_specs=(rows, P(), P(), P(), P(), rows, P()), out_specs=rows, check_vma=False
    )
```

profile of v0, /device:TPU:1, one launch (start us, length us, event | category | flops | bytes accessed | tf_op | source)
XLA Modules:
  0.0 117.2 jit_solution(14378481762099823869)
XLA Ops:
  0.0 9.6 %forecast.1 = (f32[2048,128]{1,0:T(8,128)}, f32[64,128]{1,0:T(8,128)}) custom-call(s32[8,128]{1,0:T(8,128)} %bitcast.18, f32[4,1024]{1,0:T(4,128)} %noise_ref.1, f32[2048,128]{1,0:T(8,128)} %bitcast.12), custom_call_target="tpu_custom_call" | custom-call | tf_op jit(solution)/shard_map/forecast/pallas_call | solution.py:352
  9.6 4.2 %collective-permute-start.2 = (f32[1,64,128]{2,1,0:T(8,128)}, f32[1,64,128]{2,1,0:T(8,128)S(1)}, u32[]{:S(2)}, u32[]{:S(2)}) collective-permute-start(f32[1,64,128]{2,1,0:T(8,128)} %bitcast.14), channel_id=1, source_target_pairs={{0,3},{1,2},{2,1},{3,0},{4,7},{5,6},{6,5},{7,4},{8,11},{9,10},{10,... | collective-permute-start | bytes 98312 | tf_op jit(solution)/shard_map/ppermute | solution.py:334
  13.8 0.0 collective-permute-start.1
  13.8 0.4 collective-permute-start
  14.2 1.2 collective-permute-done.2
  15.3 2.4 %collective-permute-done.1 = f32[1,64,128]{2,1,0:T(8,128)S(1)} collective-permute-done((f32[1,64,128]{2,1,0:T(8,128)}, f32[1,64,128]{2,1,0:T(8,128)S(1)}, u32[]{:S(2)}, u32[]{:S(2)}) %collective-permute-start.1) | collective-permute-done | bytes 32800 | tf_op jit(solution)/shard_map/ppermute | solution.py:334
  17.7 0.0 collective-permute-done
  17.7 0.8 pad_maximum_fusion.1.refs_0_
  18.4 6.1 %all-to-all-start = ((f32[32,64,128]{2,1,0:T(8,128)}), f32[32,64,128]{2,1,0:T(8,128)S(1)}, u32[]{:S(2)}, u32[]{:S(2)}) async-start(f32[32,64,128]{2,1,0:T(8,128)} %bitcast.13), calls=%async_computation | async-start | bytes 2097152 | tf_op jit(solution)/shard_map/all_to_all | solution.py:376
  24.6 2.3 %collective-permute-start.6 = (f32[4,64,128]{2,1,0:T(8,128)S(1)}, f32[4,64,128]{2,1,0:T(8,128)S(1)}, u32[]{:S(2)}, u32[]{:S(2)}) collective-permute-start(f32[4,64,128]{2,1,0:T(8,128)S(1)} %pad_maximum_fusion.1.refs_0_), channel_id=1, source_target_pairs={{0,24},{1,25},{2,26},{3,27},{4,28},{5,29},{6,30},{7,31},{8,16},{9,... | collective-permute-start | bytes 393224 | tf_op jit(solution)/shard_map/ppermute | solution.py:334
  26.9 0.3 collective-permute-start.5
  27.2 0.1 collective-permute-start.4
  27.3 11.0 %collective-permute-done.6.refs_4_ = f32[4,64,128]{2,1,0:T(8,128)S(1)} collective-permute-done((f32[4,64,128]{2,1,0:T(8,128)S(1)}, f32[4,64,128]{2,1,0:T(8,128)S(1)}, u32[]{:S(2)}, u32[]{:S(2)}) %collective-permute-start.6) | collective-permute-done | bytes 131104 | tf_op jit(solution)/shard_map/ppermute | solution.py:334
  38.3 2.9 %collective-permute-done.5.refs_3_ = f32[4,64,128]{2,1,0:T(8,128)S(1)} collective-permute-done((f32[4,64,128]{2,1,0:T(8,128)S(1)}, f32[4,64,128]{2,1,0:T(8,128)S(1)}, u32[]{:S(2)}, u32[]{:S(2)}) %collective-permute-start.5) | collective-permute-done | bytes 131104 | tf_op jit(solution)/shard_map/ppermute | solution.py:334
  41.2 1.4 %collective-permute-start.7 = (f32[12,64,128]{2,1,0:T(8,128)S(1)}, f32[12,64,128]{2,1,0:T(8,128)S(1)}, u32[]{:S(2)}, u32[]{:S(2)}) collective-permute-start(f32[12,64,128]{2,1,0:T(8,128)S(1)} %pad_maximum_fusion), channel_id=1, source_target_pairs={{0,4},{1,5},{2,6},{3,7},{4,0},{5,1},{6,2},{7,3},{8,12},{9,13},{10,... | collective-permute-start | bytes 1179656 | tf_op jit(solution)/shard_map/ppermute | solution.py:334
  42.5 0.1 collective-permute-start.3
  42.6 2.1 %prepare.1 = (bf16[4,1024,128]{2,1,0:T(8,128)(2,1)}, f32[4,128]{1,0:T(4,128)}) custom-call(s32[1]{0:T(128)S(6)} %mul.7.zone_ref, s32[128,128]{1,0:T(8,128)} %neighbours_ref.1, f32[1,1024]{1,0:T(1,128)} %bitcast.20, s32[1,1024]{1,0:T(1,128)} %bitcast.19), custom_call_target="tpu_custom_call" | custom-call | tf_op jit(solution)/shard_map/prepare/pallas_call | solution.py:338
  44.7 0.0 collective-permute-done.7.refs_5_
  44.7 11.8 %solve.1.transform_ref = f32[4,128,128]{2,1,0:T(8,128)} custom-call(s32[1]{0:T(128)} %bitcast.me_ref, bf16[4,1024,128]{2,1,0:T(8,128)(2,1)} %get-tuple-element.11.pick_ref, f32[4,128]{1,0:T(4,128)} %get-tuple-element.12.errors_ref, f32[1,1024]{1,0:T(1,128)} %bitcast.22, f32[1,1024]{1,0:T(1,128)} %bitcast.21, f32[4,64,128]{2,1,0:T(8,128)S(1)} %pad_maximum_fusion.1.refs_0_, ...), custom_call_target="tpu_custom_call" | custom-call | tf_op jit(solution)/shard_map/solve/pallas_call | solution.py:383
  56.6 3.3 %analyse.1 = f32[32,128,128]{2,1,0:T(8,128)} custom-call(s32[32]{0:T(128)} %counts_ref.1, f32[4,128,128]{2,1,0:T(8,128)} %solve.1.transform_ref, f32[32,64,128]{2,1,0:T(8,128)S(1)} %all-to-all-done.cells_ref), custom_call_target="tpu_custom_call" | custom-call | tf_op jit(solution)/shard_map/analyse/pallas_call | solution.py:396
  59.9 5.2 %all-to-all-start.1 = ((f32[32,128,128]{2,1,0:T(8,128)}), f32[32,128,128]{2,1,0:T(8,128)S(1)}, u32[]{:S(2)}, u32[]{:S(2)}) async-start(f32[32,128,128]{2,1,0:T(8,128)} %analyse.1), calls=%async_computation.1 | async-start | bytes 4194304 | tf_op jit(solution)/shard_map/all_to_all | solution.py:407
  65.2 0.6 dynamic_slice.3.count_ref
  65.8 47.7 %all-to-all-done.1.rows_ref = f32[32,128,128]{2,1,0:T(8,128)S(1)} async-done(((f32[32,128,128]{2,1,0:T(8,128)}), f32[32,128,128]{2,1,0:T(8,128)S(1)}, u32[]{:S(2)}, u32[]{:S(2)}) %all-to-all-start.1) | async-done | bytes 2097184 | tf_op jit(solution)/shard_map/all_to_all | solution.py:407
  113.5 3.7 %advance.1 = f32[8,65536]{1,0:T(8,128)} custom-call(s32[1]{0:T(128)} %dynamic_slice.3.count_ref, f32[32,128,128]{2,1,0:T(8,128)S(1)} %all-to-all-done.1.rows_ref), custom_call_target="tpu_custom_call" | custom-call | tf_op jit(solution)/shard_map/advance/pallas_call | solution.py:410
  (6 shorter events, 0.0 us)
Async XLA Ops:
  9.6 5.7 %collective-permute-start.2 = (f32[1,64,128]{2,1,0:T(8,128)}, f32[1,64,128]{2,1,0:T(8,128)S(1)}, u32[]{:S(2)}, u32[]{:S(2)}) collective-permute-start(f32[1,64,128]{2,1,0:T(8,128)} %bitcast.14), channel_id=1, source_target_pairs={{0,3},{1,2},{2,1},{3,0},{4,7},{5,6},{6,5},{7,4},{8,11},{9,10},{10,... | collective-permute-start | bytes 98312 | tf_op jit(solution)/shard_map/ppermute | solution.py:334
  13.8 3.9 %collective-permute-start.1 = (f32[1,64,128]{2,1,0:T(8,128)}, f32[1,64,128]{2,1,0:T(8,128)S(1)}, u32[]{:S(2)}, u32[]{:S(2)}) collective-permute-start(f32[1,64,128]{2,1,0:T(8,128)} %bitcast.15), channel_id=1, source_target_pairs={{0,2},{1,3},{2,0},{3,1},{4,6},{5,7},{6,4},{7,5},{8,10},{9,11},{10,... | collective-permute-start | bytes 98312 | tf_op jit(solution)/shard_map/ppermute | solution.py:334
  13.8 3.9 %collective-permute-start = (f32[1,64,128]{2,1,0:T(8,128)}, f32[1,64,128]{2,1,0:T(8,128)S(1)}, u32[]{:S(2)}, u32[]{:S(2)}) collective-permute-start(f32[1,64,128]{2,1,0:T(8,128)} %bitcast.16), channel_id=1, source_target_pairs={{0,1},{1,0},{2,3},{3,2},{4,5},{5,4},{6,7},{7,6},{8,9},{9,8},{10,11... | collective-permute-start | bytes 98312 | tf_op jit(solution)/shard_map/ppermute | solution.py:334
  18.4 38.2 %all-to-all-start = ((f32[32,64,128]{2,1,0:T(8,128)}), f32[32,64,128]{2,1,0:T(8,128)S(1)}, u32[]{:S(2)}, u32[]{:S(2)}) async-start(f32[32,64,128]{2,1,0:T(8,128)} %bitcast.13), calls=%async_computation | async-start | bytes 2097152 | tf_op jit(solution)/shard_map/all_to_all | solution.py:376
  24.6 13.7 %collective-permute-start.6 = (f32[4,64,128]{2,1,0:T(8,128)S(1)}, f32[4,64,128]{2,1,0:T(8,128)S(1)}, u32[]{:S(2)}, u32[]{:S(2)}) collective-permute-start(f32[4,64,128]{2,1,0:T(8,128)S(1)} %pad_maximum_fusion.1.refs_0_), channel_id=1, source_target_pairs={{0,24},{1,25},{2,26},{3,27},{4,28},{5,29},{6,30},{7,31},{8,16},{9,... | collective-permute-start | bytes 393224 | tf_op jit(solution)/shard_map/ppermute | solution.py:334
  26.9 14.3 %collective-permute-start.5 = (f32[4,64,128]{2,1,0:T(8,128)S(1)}, f32[4,64,128]{2,1,0:T(8,128)S(1)}, u32[]{:S(2)}, u32[]{:S(2)}) collective-permute-start(f32[4,64,128]{2,1,0:T(8,128)S(1)} %pad_maximum_fusion.1.refs_0_), channel_id=1, source_target_pairs={{0,16},{1,17},{2,18},{3,19},{4,20},{5,21},{6,22},{7,23},{8,24},{9,... | collective-permute-start | bytes 393224 | tf_op jit(solution)/shard_map/ppermute | solution.py:334
  27.2 14.0 %collective-permute-start.4 = (f32[4,64,128]{2,1,0:T(8,128)S(1)}, f32[4,64,128]{2,1,0:T(8,128)S(1)}, u32[]{:S(2)}, u32[]{:S(2)}) collective-permute-start(f32[4,64,128]{2,1,0:T(8,128)S(1)} %pad_maximum_fusion.1.refs_0_), channel_id=1, source_target_pairs={{0,8},{1,9},{2,10},{3,11},{4,12},{5,13},{6,14},{7,15},{8,0},{9,1},... | collective-permute-start | bytes 393224 | tf_op jit(solution)/shard_map/ppermute | solution.py:334
  41.2 3.6 %collective-permute-start.7 = (f32[12,64,128]{2,1,0:T(8,128)S(1)}, f32[12,64,128]{2,1,0:T(8,128)S(1)}, u32[]{:S(2)}, u32[]{:S(2)}) collective-permute-start(f32[12,64,128]{2,1,0:T(8,128)S(1)} %pad_maximum_fusion), channel_id=1, source_target_pairs={{0,4},{1,5},{2,6},{3,7},{4,0},{5,1},{6,2},{7,3},{8,12},{9,13},{10,... | collective-permute-start | bytes 1179656 | tf_op jit(solution)/shard_map/ppermute | solution.py:334
  42.5 2.2 %collective-permute-start.3 = (f32[4,64,128]{2,1,0:T(8,128)S(1)}, f32[4,64,128]{2,1,0:T(8,128)S(1)}, u32[]{:S(2)}, u32[]{:S(2)}) collective-permute-start(f32[4,64,128]{2,1,0:T(8,128)S(1)} %pad_maximum_fusion.1.refs_0_), channel_id=1, source_target_pairs={{0,4},{1,5},{2,6},{3,7},{4,0},{5,1},{6,2},{7,3},{8,12},{9,13},{10,... | collective-permute-start | bytes 393224 | tf_op jit(solution)/shard_map/ppermute | solution.py:334
  59.9 5.3 %copy-start = (s32[32]{0:T(128)S(1)}, s32[32]{0:T(128)}, u32[]{:S(2)}) copy-start(s32[32]{0:T(128)} %counts_ref.1) | copy-start | bytes 388
  59.9 53.6 %all-to-all-start.1 = ((f32[32,128,128]{2,1,0:T(8,128)}), f32[32,128,128]{2,1,0:T(8,128)S(1)}, u32[]{:S(2)}, u32[]{:S(2)}) async-start(f32[32,128,128]{2,1,0:T(8,128)} %analyse.1), calls=%async_computation.1 | async-start | bytes 4194304 | tf_op jit(solution)/shard_map/all_to_all | solution.py:407
where the time goes:
time: 118 us; the launch traced here: 117 us
  waiting for transfers between devices  65.1 us (55%)
  Pallas kernels  30.6 us (26%)
  starting transfers between devices  20.1 us (17%)
    all_to_all x1, waiting for transfers between devices, per_device(): owned = exchange(outgoing)  47.7 us
    ppermute x8, waiting for transfers between devices, swap(): lax.ppermute(value, AXES, [(device, device ^ bits) for device in range(de...  17.4 us
    pallas_call x1, Pallas kernels, per_device(): pl.pallas_call(functools.partial(solve_kernel, masks=masks), out_shape=ja...  11.8 us
    pallas_call x1, Pallas kernels, per_device(): pl.pallas_call(functools.partial(forecast_kernel, members=members), out_s...  9.58 us
    ppermute x8, starting transfers between devices, swap(): lax.ppermute(value, AXES, [(device, device ^ bits) for device in range(de...  8.72 us
    all_to_all x1, starting transfers between devices, per_device(): own_cells = exchange(state.reshape(devices, height // devices, LANES))  6.12 us
    all_to_all x1, starting transfers between devices, per_device(): owned = exchange(outgoing)  5.25 us
    pallas_call x1, Pallas kernels, per_device(): pl.pallas_call(advance_kernel, grid=(steps,), out_shape=jax.ShapeDtypeStr...  3.7 us
  transfers between devices with their start and end apart: 10, of which 5 were waited for; matrix products, arithmetic and copies ran while one was open for 1% of the time, Pallas kernels for 12%

commit v1 on v0

--- a/solution.py
+++ b/solution.py
@@ -28,7 +28,7 @@
     return lax.broadcasted_iota(jnp.int32, (ROWS, LANES), 0)
 
 
-def forecast_kernel(places_ref, noise_ref, x_ref, state_ref, mine_ref, tile_ref, table_ref, scalar_ref, table_sem, *, members):
+def forecast_kernel(places_ref, noise_ref, x_ref, out_ref, mine_ref, rows_ref, state_ref, tile_ref, table_ref, scalar_ref, table_sem, in_sem, out_sem, *, members):
     height = x_ref.shape[0]
     blocks = places_ref.shape[0]
     tiles = height // LANES
@@ -42,8 +42,15 @@
     def group(cell):
         return [state_ref[cell * tiles + half * ROWS : cell * tiles + (half + 1) * ROWS, :] for half in range(halves)]
 
-    for tile in range(tiles):
-        tile_ref[tile * tile_pitch : tile * tile_pitch + LANES, :] = (x_ref[tile * LANES : (tile + 1) * LANES, :] * TIME_STEP).T
+    def tile_rows(tile):
+        return slice(tile * LANES, (tile + 1) * LANES)
+
+    incoming = [pltpu.make_async_copy(x_ref.at[tile_rows(tile)], rows_ref.at[tile_rows(tile)], in_sem.at[tile]) for tile in range(tiles)]
+    for copy in incoming:
+        copy.start()
+    for tile, copy in enumerate(incoming):
+        copy.wait()
+        tile_ref[tile * tile_pitch : tile * tile_pitch + LANES, :] = (rows_ref[tile_rows(tile), :] * TIME_STEP).T
     for cell in range(LANES):
         for half in range(halves):
             begin = cell * tiles + half * ROWS
@@ -100,15 +107,17 @@
         for half in range(halves):
             begin = cell * cell_pitch + half * ROWS
             tile_ref[begin : begin + ROWS, :] = group(cell)[half]
-    for tile in range(tiles):
-        state_ref[tile * LANES : (tile + 1) * LANES, :] = tile_ref[pl.ds(tile, LANES, stride=cell_pitch), :].T * (1.0 / TIME_STEP)
+    outgoing = [pltpu.make_async_copy(rows_ref.at[tile_rows(tile)], out_ref.at[tile_rows(tile)], out_sem.at[tile]) for tile in range(tiles)]
+    for tile, copy in enumerate(outgoing):
+        rows_ref[tile_rows(tile), :] = tile_ref[pl.ds(tile, LANES, stride=cell_pitch), :].T * (1.0 / TIME_STEP)
+        copy.start()
     table_copy.wait()
 
     def gather(block, carry):
         picked = [jnp.zeros((ROWS, LANES), jnp.float32) for _ in range(4)]
         for number in range(LANES):
             begin = pl.multiple_of(scalar_ref[block, number], ROWS)
-            turned = pltpu.roll(state_ref[pl.ds(begin, ROWS), :], scalar_ref[blocks + block, number], axis=1)
+            turned = pltpu.roll(rows_ref[pl.ds(begin, ROWS), :], scalar_ref[blocks + block, number], axis=1)
             picked[number % 4] = jnp.where(lane == number, turned, picked[number % 4])
         both = picked[0]
         for number in range(1, 4):
@@ -124,6 +133,8 @@
     for block in range(blocks):
         begin = (blocks + block) * members
         mine_ref[begin : begin + members, :] = noise_ref[:, block * LANES : (block + 1) * LANES]
+    for copy in outgoing:
+        copy.wait()
 
 
 def dot(a, b, contract, precision=HIGH):
@@ -137,49 +148,67 @@
     return high, middle, (rest - middle.astype(jnp.float32)).astype(jnp.bfloat16)
 
 
-def invert_all(matrix_ref):
-    regions, size, _ = matrix_ref.shape
+def invert_all(matrix_refs, left_refs, right_refs, done_refs):
+    regions = len(matrix_refs)
+    size = matrix_refs[0].shape[0]
+    panels = size // ROWS
     lane = lanes_iota()
     row = rows_iota()
 
-    def panel(number, carry):
-        base = number * ROWS
-        start = pl.multiple_of(base, ROWS)
-        offset = lane - base
-        inside = (offset >= 0) & (offset < ROWS)
+    def inside(number):
+        offset = lane - number * ROWS
+        return (offset >= 0) & (offset < ROWS)
+
+    def rows_of(number):
+        return pl.ds(pl.multiple_of(number * ROWS, ROWS), ROWS)
+
+    def add_products(group, number):
+        for region in group:
+            update = dot(left_refs[region][...], right_refs[region][...], ((0,), (0,)), lax.Precision.DEFAULT)
+            for i in range(panels):
+                rows = slice(i * ROWS, (i + 1) * ROWS)
+                matrix_refs[region][rows, :] = jnp.where(inside(number), 0.0, matrix_refs[region][rows, :]) + update[rows]
+            matrix_refs[region][rows_of(number), :] = done_refs[region][...]
+
+    def eliminate(group, number):
+        offset = lane - number * ROWS
+        here = inside(number)
         unit = jnp.where(offset == row, 1.0, 0.0)
-        blocks = [matrix_ref[region, pl.ds(start, ROWS), :] for region in range(regions)]
+        blocks = {region: matrix_refs[region][rows_of(number), :] for region in group}
         columns = []
         for k in range(ROWS):
-            index = jnp.full((ROWS, LANES), base + k, jnp.int32)
-            columns.append([jnp.take_along_axis(block, index, axis=1) for block in blocks])
-        lefts = []
-        for block in blocks:
-            signed = jnp.where(inside, 0.0, jnp.where(offset < 0, block, -block))
-            high, middle, low = split_three(signed)
-            lefts.append(jnp.concatenate([high, high, middle, high, low, middle], axis=0))
-        blocks = [jnp.where(inside, unit, block) for block in blocks]
+            index = jnp.full((ROWS, LANES), number * ROWS + k, jnp.int32)
+            columns.append({region: jnp.take_along_axis(blocks[region], index, axis=1) for region in group})
+        for region in group:
+            high, middle, low = split_three(jnp.where(here, 0.0, jnp.where(offset < 0, blocks[region], -blocks[region])))
+            left_refs[region][...] = jnp.concatenate([high, high, middle, high, low, middle], axis=0)
+            blocks[region] = jnp.where(here, unit, blocks[region])
         for j in range(ROWS):
-            here = row == j
-            for region in range(regions):
+            at = row == j
+            for region in group:
                 pivot = columns[j][region]
                 inverse = 1.0 / pivot[j : j + 1, :]
                 scaled = blocks[region][j : j + 1, :] * inverse
-                blocks[region] = jnp.where(here, scaled, blocks[region] - pivot * scaled)
+                blocks[region] = jnp.where(at, scaled, blocks[region] - pivot * scaled)
                 for k in range(j + 1, ROWS):
                     scaled = columns[k][region][j : j + 1, :] * inverse
-                    columns[k][region] = jnp.where(here, scaled, columns[k][region] - pivot * scaled)
-        for region in range(regions):
+                    columns[k][region] = jnp.where(at, scaled, columns[k][region] - pivot * scaled)
+        for region in group:
+            done_refs[region][...] = blocks[region]
             high, middle, low = split_three(blocks[region])
-            right = jnp.concatenate([high, middle, high, low, high, middle], axis=0)
-            update = dot(lefts[region], right, ((0,), (0,)), lax.Precision.DEFAULT)
-            for i in range(size // ROWS):
-                rows = slice(i * ROWS, (i + 1) * ROWS)
-                matrix_ref[region, rows, :] = jnp.where(inside, 0.0, matrix_ref[region, rows, :]) + update[rows]
-            matrix_ref[region, pl.ds(start, ROWS), :] = blocks[region]
+            right_refs[region][...] = jnp.concatenate([high, middle, high, low, high, middle], axis=0)
+
+    def panel(number, carry):
+        eliminate(range(regions), number)
+        add_products(range(regions), number)
         return carry
 
-    lax.fori_loop(0, size // ROWS, panel, 0)
+    lax.fori_loop(0, panels, panel, 0)
+
+
+def invert_scratch(regions, size):
+    factor = pltpu.VMEM((6 * ROWS, size), jnp.bfloat16)
+    return [[pltpu.VMEM((size, size), jnp.float32)] * regions, [factor] * regions, [factor] * regions, [pltpu.VMEM((ROWS, size), jnp.float32)] * regions]
 
 
 def split_two(value):
@@ -212,7 +241,7 @@
 
 
 def solve_kernel(me_ref, pick_ref, errors_ref, values_ref, variance_ref, *refs, masks):
-    *blocks_refs, transform_ref, stack_ref, pieces_ref, matrix_ref = refs
+    *blocks_refs, transform_ref, stack_ref, pieces_ref, matrix_refs, left_refs, right_refs, done_refs = refs
     regions, total, _ = transform_ref.shape
     observations = values_ref.shape[1]
     blocks = observations // LANES
@@ -240,15 +269,15 @@
         innovations.append(picked[total:])
         anomaly = equivalents - jnp.sum(equivalents, axis=0, keepdims=True) * (1.0 / total)
         anomalies.append(anomaly)
-        covariance = dot(anomaly, anomaly, ((0,), (0,))) * (1.0 / (total - 1))
-        matrix_ref[region, :, :] = jnp.where(diagonal, covariance + errors_ref[region : region + 1, :], covariance)
-    invert_all(matrix_ref)
+        covariance = dot(anomaly.T, anomaly, ((1,), (0,))) * (1.0 / (total - 1))
+        matrix_refs[region][...] = jnp.where(diagonal, covariance + errors_ref[region : region + 1, :], covariance)
+    invert_all(matrix_refs, left_refs, right_refs, done_refs)
     for region in range(regions):
-        weights = dot_split(innovations[region], matrix_ref[region], ((1,), (0,)))
+        weights = dot_split(innovations[region], matrix_refs[region][...], ((1,), (0,)))
         transform_ref[region, :, :] = dot_split(weights, anomalies[region], ((1,), (1,))) * (1.0 / (total - 1))
 
 
-def apply_kernel(counts_ref, transform_ref, cells_ref, owned_ref, block_ref, result_ref):
+def apply_kernel(counts_ref, transform_ref, cells_ref, owned_ref, block_ref, result_ref, staging_ref, out_sem):
     sources, height, _ = cells_ref.shape
     regions, total, _ = transform_ref.shape
     members = total // sources
@@ -269,41 +298,64 @@
 
     def window(destination, offset):
         for tile in range(tiles):
-            owned_ref[destination, tile * ROWS : (tile + 1) * ROWS, :] = result_ref[tile, pl.ds(offset, CAP), :]
+            staging_ref[destination, tile * ROWS : (tile + 1) * ROWS, :] = result_ref[tile, pl.ds(offset, CAP), :]
         return offset + counts_ref[destination]
 
-    lax.fori_loop(0, sources, window, jnp.int32(0))
-
-
-def advance_kernel(count_ref, rows_ref, out_ref):
+    groups = out_sem.shape[0]
+    group = sources // groups
+    offset = jnp.int32(0)
+    copies = []
+    for number in range(groups):
+        offset = lax.fori_loop(number * group, (number + 1) * group, window, offset)
+        span = slice(number * group, (number + 1) * group)
+        copies.append(pltpu.make_async_copy(staging_ref.at[span], owned_ref.at[span], out_sem.at[number]))
+        copies[-1].start()
+    for copy in copies:
+        copy.wait()
+
+
+def advance_kernel(count_ref, rows_ref, out_ref, staging_ref, out_sem):
     sources, height, _ = rows_ref.shape
     tiles = height // ROWS
-    here = out_ref.shape[1] // LANES // tiles
+    chunks = out_sem.shape[0]
+    here = sources // chunks
+    width = here * tiles * LANES
     lane = lanes_iota()
     occupied = rows_iota() < count_ref[0]
-    start = pl.program_id(0) * here
 
     def load(source, tile):
         return rows_ref[source, tile * ROWS : (tile + 1) * ROWS, :]
 
-    before = load(lax.rem(start + sources - 1, sources), tiles - 1)
-    before_one = pltpu.roll(before, 1, axis=1)
-    before_two = pltpu.roll(before, 2, axis=1)
-    current = load(start, 0)
-    current_up = pltpu.roll(current, LANES - 1, axis=1)
-    for number in range(here * tiles):
-        source, tile = divmod(number + 1, tiles)
-        after = load(start + source if source < here else lax.rem(start + here, sources), tile)
-        after_up = pltpu.roll(after, LANES - 1, axis=1)
-        one = pltpu.roll(current, 1, axis=1)
-        two = pltpu.roll(current, 2, axis=1)
-        left = jnp.where(lane == 0, before_one, one)
-        left_two = jnp.where(lane < 2, before_two, two)
-        right = jnp.where(lane == LANES - 1, after_up, current_up)
-        stepped = current + TIME_STEP * ((right - left_two) * left - current + FORCING)
-        out_ref[:, number * LANES : (number + 1) * LANES] = jnp.where(occupied, stepped, 0.0)
-        before_one, before_two = one, two
-        current, current_up = after, after_up
+    def out_copy(chunk):
+        lanes = pl.ds(pl.multiple_of(chunk * width, width), width)
+        return pltpu.make_async_copy(staging_ref.at[chunk], out_ref.at[:, lanes], out_sem.at[chunk])
+
+    def step(chunk, carry):
+        start = chunk * here
+        before = load(lax.rem(start + sources - 1, sources), tiles - 1)
+        before_one = pltpu.roll(before, 1, axis=1)
+        before_two = pltpu.roll(before, 2, axis=1)
+        current = load(start, 0)
+        current_up = pltpu.roll(current, LANES - 1, axis=1)
+        for number in range(here * tiles):
+            source, tile = divmod(number + 1, tiles)
+            after = load(start + source if source < here else lax.rem(start + here, sources), tile)
+            after_up = pltpu.roll(after, LANES - 1, axis=1)
+            one = pltpu.roll(current, 1, axis=1)
+            two = pltpu.roll(current, 2, axis=1)
+            left = jnp.where(lane == 0, before_one, one)
+            left_two = jnp.where(lane < 2, before_two, two)
+            right = jnp.where(lane == LANES - 1, after_up, current_up)
+            stepped = current + TIME_STEP * ((right - left_two) * left - current + FORCING)
+            staging_ref[chunk, :, number * LANES : (number + 1) * LANES] = jnp.where(occupied, stepped, 0.0)
+            before_one, before_two = one, two
+            current, current_up = after, after_up
+        out_copy(chunk).start()
+        return carry
+
+    lax.fori_loop(0, chunks, step, 0)
+    for chunk in range(chunks):
+        out_copy(chunk).wait()
 
 
 def whole(space=pltpu.VMEM):
@@ -355,13 +407,17 @@
             jax.ShapeDtypeStruct((height, LANES), jnp.float32),
             jax.ShapeDtypeStruct((2 * blocks * members, LANES), jnp.float32),
         ),
-        in_specs=[whole()] * 3,
-        out_specs=(whole(),) * 2,
+        in_specs=[whole(), whole(), whole(pltpu.HBM)],
+        out_specs=(whole(pltpu.HBM), whole()),
         scratch_shapes=[
+            pltpu.VMEM((height, LANES), jnp.float32),
+            pltpu.VMEM((height, LANES), jnp.float32),
             pltpu.VMEM((max(tiles * (LANES + ROWS), LANES * (tiles + ROWS)), LANES), jnp.float32),
             pltpu.VMEM((2 * blocks, LANES), jnp.int32),
             pltpu.SMEM((2 * blocks, LANES), jnp.int32),
             pltpu.SemaphoreType.DMA,
+            pltpu.SemaphoreType.DMA((tiles,)),
+            pltpu.SemaphoreType.DMA((tiles,)),
         ],
         name="forecast",
     )(measured_indexes.reshape(blocks, LANES), perturbation, runs)
@@ -388,7 +444,7 @@
         scratch_shapes=[
             pltpu.VMEM((blocks, 2 * total, LANES), jnp.float32),
             pltpu.VMEM((4 * total, observations), jnp.bfloat16),
-            pltpu.VMEM((regions, local, local), jnp.float32),
+            *invert_scratch(regions, local),
         ],
         name="solve",
     )(me, pick, errors, values, variance, *map(place, pieces))
@@ -397,22 +453,24 @@
         apply_kernel,
         out_shape=jax.ShapeDtypeStruct((devices, share_tiles * CAP, LANES), jnp.float32),
         in_specs=[whole(pltpu.SMEM), whole(), whole()],
-        out_specs=whole(),
+        out_specs=whole(pltpu.HBM),
         scratch_shapes=[
             pltpu.VMEM((total, share_tiles * LANES), jnp.float32),
             pltpu.VMEM((share_tiles, total + ROWS, LANES), jnp.float32),
+            pltpu.VMEM((devices, share_tiles * CAP, LANES), jnp.float32),
+            pltpu.SemaphoreType.DMA((4,)),
         ],
         name="analyse",
     )(counts, transform, in_vmem(own_cells))
     owned = exchange(outgoing)
 
-    steps = 4
+    chunks = 8
     return pl.pallas_call(
         advance_kernel,
-        grid=(steps,),
         out_shape=jax.ShapeDtypeStruct((CAP, cells), jnp.float32),
         in_specs=[whole(pltpu.SMEM), whole()],
-        out_specs=pl.BlockSpec((CAP, cells // steps), lambda i: (0, i)),
+        out_specs=whole(pltpu.HBM),
+        scratch_shapes=[pltpu.VMEM((chunks, CAP, cells // chunks), jnp.float32), pltpu.SemaphoreType.DMA((chunks,))],
         name="advance",
     )(lax.dynamic_slice_in_dim(counts, device_index, 1, 0), in_vmem(owned))
 

time: 118 us -> 119 us (level)
  Pallas kernels: 30.6 us -> 32.1 us
    pallas_call x1, Pallas kernels: 9.58 us -> 11.2 us  [per_device(): pl.pallas_call(functools.partial(forecast_kernel, members=members), out_s...]
where the time goes in v1:
time: 119 us
  waiting for transfers between devices  65.1 us (55%)
  Pallas kernels  32.1 us (27%)
  starting transfers between devices  20.1 us (17%)
    all_to_all x1, waiting for transfers between devices, per_device(): owned = exchange(outgoing)  47.7 us
    ppermute x8, waiting for transfers between devices, swap(): lax.ppermute(value, AXES, [(device, device ^ bits) for device in range(de...  17.4 us
    pallas_call x1, Pallas kernels, per_device(): pl.pallas_call(functools.partial(solve_kernel, masks=masks), out_shape=ja...  11.9 us
    pallas_call x1, Pallas kernels, per_device(): pl.pallas_call(functools.partial(forecast_kernel, members=members), out_s...  11.2 us
    ppermute x8, starting transfers between devices, swap(): lax.ppermute(value, AXES, [(device, device ^ bits) for device in range(de...  8.72 us
    all_to_all x1, starting transfers between devices, per_device(): own_cells = exchange(state.reshape(devices, height // devices, LANES))  6.12 us
    all_to_all x1, starting transfers between devices, per_device(): owned = exchange(outgoing)  5.25 us
    pallas_call x1, Pallas kernels, per_device(): pl.pallas_call(advance_kernel, out_shape=jax.ShapeDtypeStruct((CAP, cells...  3.65 us
  transfers between devices with their start and end apart: 10, of which 5 were waited for; matrix products, arithmetic and copies ran while one was open for 1% of the time, Pallas kernels for 12%

profile of v1, /device:TPU:1, one launch (start us, length us, event | category | flops | bytes accessed | tf_op | source)
XLA Modules:
  0.0 118.7 jit_solution(9910602930032845383)
XLA Ops:
  0.0 11.2 %forecast.1 = (f32[2048,128]{1,0:T(8,128)}, f32[64,128]{1,0:T(8,128)}) custom-call(s32[8,128]{1,0:T(8,128)} %bitcast.18, f32[4,1024]{1,0:T(4,128)} %noise_ref.1, f32[2048,128]{1,0:T(8,128)} %bitcast.12), custom_call_target="tpu_custom_call" | custom-call | tf_op jit(solution)/shard_map/forecast/pallas_call | solution.py:404
  11.3 4.2 %collective-permute-start.2 = (f32[1,64,128]{2,1,0:T(8,128)}, f32[1,64,128]{2,1,0:T(8,128)S(1)}, u32[]{:S(2)}, u32[]{:S(2)}) collective-permute-start(f32[1,64,128]{2,1,0:T(8,128)} %bitcast.14), channel_id=1, source_target_pairs={{0,3},{1,2},{2,1},{3,0},{4,7},{5,6},{6,5},{7,4},{8,11},{9,10},{10,... | collective-permute-start | bytes 98312 | tf_op jit(solution)/shard_map/ppermute | solution.py:386
  15.5 0.4 collective-permute-start
  15.8 1.2 collective-permute-done.2
  17.0 2.4 %collective-permute-done.1 = f32[1,64,128]{2,1,0:T(8,128)S(1)} collective-permute-done((f32[1,64,128]{2,1,0:T(8,128)}, f32[1,64,128]{2,1,0:T(8,128)S(1)}, u32[]{:S(2)}, u32[]{:S(2)}) %collective-permute-start.1) | collective-permute-done | bytes 32800 | tf_op jit(solution)/shard_map/ppermute | solution.py:386
  19.3 0.8 pad_maximum_fusion.1.refs_0_
  20.1 6.1 %all-to-all-start = ((f32[32,64,128]{2,1,0:T(8,128)}), f32[32,64,128]{2,1,0:T(8,128)S(1)}, u32[]{:S(2)}, u32[]{:S(2)}) async-start(f32[32,64,128]{2,1,0:T(8,128)} %bitcast.13), calls=%async_computation | async-start | bytes 2097152 | tf_op jit(solution)/shard_map/all_to_all | solution.py:432
  26.2 2.3 %collective-permute-start.6 = (f32[4,64,128]{2,1,0:T(8,128)S(1)}, f32[4,64,128]{2,1,0:T(8,128)S(1)}, u32[]{:S(2)}, u32[]{:S(2)}) collective-permute-start(f32[4,64,128]{2,1,0:T(8,128)S(1)} %pad_maximum_fusion.1.refs_0_), channel_id=1, source_target_pairs={{0,24},{1,25},{2,26},{3,27},{4,28},{5,29},{6,30},{7,31},{8,16},{9,... | collective-permute-start | bytes 393224 | tf_op jit(solution)/shard_map/ppermute | solution.py:386
  28.6 0.3 collective-permute-start.5
  28.8 0.1 collective-permute-start.4
  29.0 11.0 %collective-permute-done.6.refs_4_ = f32[4,64,128]{2,1,0:T(8,128)S(1)} collective-permute-done((f32[4,64,128]{2,1,0:T(8,128)S(1)}, f32[4,64,128]{2,1,0:T(8,128)S(1)}, u32[]{:S(2)}, u32[]{:S(2)}) %collective-permute-start.6) | collective-permute-done | bytes 131104 | tf_op jit(solution)/shard_map/ppermute | solution.py:386
  39.9 2.9 %collective-permute-done.5.refs_3_ = f32[4,64,128]{2,1,0:T(8,128)S(1)} collective-permute-done((f32[4,64,128]{2,1,0:T(8,128)S(1)}, f32[4,64,128]{2,1,0:T(8,128)S(1)}, u32[]{:S(2)}, u32[]{:S(2)}) %collective-permute-start.5) | collective-permute-done | bytes 131104 | tf_op jit(solution)/shard_map/ppermute | solution.py:386
  42.8 0.0 collective-permute-done.4.refs_2_
  42.9 1.4 %collective-permute-start.7 = (f32[12,64,128]{2,1,0:T(8,128)S(1)}, f32[12,64,128]{2,1,0:T(8,128)S(1)}, u32[]{:S(2)}, u32[]{:S(2)}) collective-permute-start(f32[12,64,128]{2,1,0:T(8,128)S(1)} %pad_maximum_fusion), channel_id=1, source_target_pairs={{0,4},{1,5},{2,6},{3,7},{4,0},{5,1},{6,2},{7,3},{8,12},{9,13},{10,... | collective-permute-start | bytes 1179656 | tf_op jit(solution)/shard_map/ppermute | solution.py:386
  44.2 0.1 collective-permute-start.3
  44.3 2.1 %prepare.1 = (bf16[4,1024,128]{2,1,0:T(8,128)(2,1)}, f32[4,128]{1,0:T(4,128)}) custom-call(s32[1]{0:T(128)S(6)} %mul.7.zone_ref, s32[128,128]{1,0:T(8,128)} %neighbours_ref.1, f32[1,1024]{1,0:T(1,128)} %bitcast.20, s32[1,1024]{1,0:T(1,128)} %bitcast.19), custom_call_target="tpu_custom_call" | custom-call | tf_op jit(solution)/shard_map/prepare/pallas_call | solution.py:390
  46.4 0.0 collective-permute-done.3.refs_1_
  46.4 11.9 %solve.1.transform_ref = f32[4,128,128]{2,1,0:T(8,128)} custom-call(s32[1]{0:T(128)} %bitcast.me_ref, bf16[4,1024,128]{2,1,0:T(8,128)(2,1)} %get-tuple-element.11.pick_ref, f32[4,128]{1,0:T(4,128)} %get-tuple-element.12.errors_ref, f32[1,1024]{1,0:T(1,128)} %bitcast.22, f32[1,1024]{1,0:T(1,128)} %bitcast.21, f32[4,64,128]{2,1,0:T(8,128)S(1)} %pad_maximum_fusion.1.refs_0_, ...), custom_call_target="tpu_custom_call" | custom-call | tf_op jit(solution)/shard_map/solve/pallas_call | solution.py:439
  58.3 3.1 %analyse.1 = f32[32,128,128]{2,1,0:T(8,128)} custom-call(s32[32]{0:T(128)} %counts_ref.1, f32[4,128,128]{2,1,0:T(8,128)} %solve.1.transform_ref, f32[32,64,128]{2,1,0:T(8,128)S(1)} %all-to-all-done.cells_ref), custom_call_target="tpu_custom_call" | custom-call | tf_op jit(solution)/shard_map/analyse/pallas_call | solution.py:452
  61.5 0.0 copy-start
  61.5 5.3 %all-to-all-start.1 = ((f32[32,128,128]{2,1,0:T(8,128)}), f32[32,128,128]{2,1,0:T(8,128)S(1)}, u32[]{:S(2)}, u32[]{:S(2)}) async-start(f32[32,128,128]{2,1,0:T(8,128)} %analyse.1), calls=%async_computation.1 | async-start | bytes 4194304 | tf_op jit(solution)/shard_map/all_to_all | solution.py:465
  66.8 0.6 dynamic_slice.3.count_ref
  67.4 47.7 %all-to-all-done.1.rows_ref = f32[32,128,128]{2,1,0:T(8,128)S(1)} async-done(((f32[32,128,128]{2,1,0:T(8,128)}), f32[32,128,128]{2,1,0:T(8,128)S(1)}, u32[]{:S(2)}, u32[]{:S(2)}) %all-to-all-start.1) | async-done | bytes 2097184 | tf_op jit(solution)/shard_map/all_to_all | solution.py:465
  115.1 3.7 %advance.1 = f32[8,65536]{1,0:T(8,128)} custom-call(s32[1]{0:T(128)} %dynamic_slice.3.count_ref, f32[32,128,128]{2,1,0:T(8,128)S(1)} %all-to-all-done.1.rows_ref), custom_call_target="tpu_custom_call" | custom-call | tf_op jit(solution)/shard_map/advance/pallas_call | solution.py:468
  (6 shorter events, 0.0 us)
Async XLA Ops:
  11.3 5.7 %collective-permute-start.2 = (f32[1,64,128]{2,1,0:T(8,128)}, f32[1,64,128]{2,1,0:T(8,128)S(1)}, u32[]{:S(2)}, u32[]{:S(2)}) collective-permute-start(f32[1,64,128]{2,1,0:T(8,128)} %bitcast.14), channel_id=1, source_target_pairs={{0,3},{1,2},{2,1},{3,0},{4,7},{5,6},{6,5},{7,4},{8,11},{9,10},{10,... | collective-permute-start | bytes 98312 | tf_op jit(solution)/shard_map/ppermute | solution.py:386
  15.5 3.9 %collective-permute-start.1 = (f32[1,64,128]{2,1,0:T(8,128)}, f32[1,64,128]{2,1,0:T(8,128)S(1)}, u32[]{:S(2)}, u32[]{:S(2)}) collective-permute-start(f32[1,64,128]{2,1,0:T(8,128)} %bitcast.15), channel_id=1, source_target_pairs={{0,2},{1,3},{2,0},{3,1},{4,6},{5,7},{6,4},{7,5},{8,10},{9,11},{10,... | collective-permute-start | bytes 98312 | tf_op jit(solution)/shard_map/ppermute | solution.py:386
  15.5 3.9 %collective-permute-start = (f32[1,64,128]{2,1,0:T(8,128)}, f32[1,64,128]{2,1,0:T(8,128)S(1)}, u32[]{:S(2)}, u32[]{:S(2)}) collective-permute-start(f32[1,64,128]{2,1,0:T(8,128)} %bitcast.16), channel_id=1, source_target_pairs={{0,1},{1,0},{2,3},{3,2},{4,5},{5,4},{6,7},{7,6},{8,9},{9,8},{10,11... | collective-permute-start | bytes 98312 | tf_op jit(solution)/shard_map/ppermute | solution.py:386
  20.1 38.2 %all-to-all-start = ((f32[32,64,128]{2,1,0:T(8,128)}), f32[32,64,128]{2,1,0:T(8,128)S(1)}, u32[]{:S(2)}, u32[]{:S(2)}) async-start(f32[32,64,128]{2,1,0:T(8,128)} %bitcast.13), calls=%async_computation | async-start | bytes 2097152 | tf_op jit(solution)/shard_map/all_to_all | solution.py:432
  26.2 13.7 %collective-permute-start.6 = (f32[4,64,128]{2,1,0:T(8,128)S(1)}, f32[4,64,128]{2,1,0:T(8,128)S(1)}, u32[]{:S(2)}, u32[]{:S(2)}) collective-permute-start(f32[4,64,128]{2,1,0:T(8,128)S(1)} %pad_maximum_fusion.1.refs_0_), channel_id=1, source_target_pairs={{0,24},{1,25},{2,26},{3,27},{4,28},{5,29},{6,30},{7,31},{8,16},{9,... | collective-permute-start | bytes 393224 | tf_op jit(solution)/shard_map/ppermute | solution.py:386
  28.6 14.3 %collective-permute-start.5 = (f32[4,64,128]{2,1,0:T(8,128)S(1)}, f32[4,64,128]{2,1,0:T(8,128)S(1)}, u32[]{:S(2)}, u32[]{:S(2)}) collective-permute-start(f32[4,64,128]{2,1,0:T(8,128)S(1)} %pad_maximum_fusion.1.refs_0_), channel_id=1, source_target_pairs={{0,16},{1,17},{2,18},{3,19},{4,20},{5,21},{6,22},{7,23},{8,24},{9,... | collective-permute-start | bytes 393224 | tf_op jit(solution)/shard_map/ppermute | solution.py:386
  28.8 14.0 %collective-permute-start.4 = (f32[4,64,128]{2,1,0:T(8,128)S(1)}, f32[4,64,128]{2,1,0:T(8,128)S(1)}, u32[]{:S(2)}, u32[]{:S(2)}) collective-permute-start(f32[4,64,128]{2,1,0:T(8,128)S(1)} %pad_maximum_fusion.1.refs_0_), channel_id=1, source_target_pairs={{0,8},{1,9},{2,10},{3,11},{4,12},{5,13},{6,14},{7,15},{8,0},{9,1},... | collective-permute-start | bytes 393224 | tf_op jit(solution)/shard_map/ppermute | solution.py:386
  42.9 3.6 %collective-permute-start.7 = (f32[12,64,128]{2,1,0:T(8,128)S(1)}, f32[12,64,128]{2,1,0:T(8,128)S(1)}, u32[]{:S(2)}, u32[]{:S(2)}) collective-permute-start(f32[12,64,128]{2,1,0:T(8,128)S(1)} %pad_maximum_fusion), channel_id=1, source_target_pairs={{0,4},{1,5},{2,6},{3,7},{4,0},{5,1},{6,2},{7,3},{8,12},{9,13},{10,... | collective-permute-start | bytes 1179656 | tf_op jit(solution)/shard_map/ppermute | solution.py:386
  44.2 2.2 %collective-permute-start.3 = (f32[4,64,128]{2,1,0:T(8,128)S(1)}, f32[4,64,128]{2,1,0:T(8,128)S(1)}, u32[]{:S(2)}, u32[]{:S(2)}) collective-permute-start(f32[4,64,128]{2,1,0:T(8,128)S(1)} %pad_maximum_fusion.1.refs_0_), channel_id=1, source_target_pairs={{0,4},{1,5},{2,6},{3,7},{4,0},{5,1},{6,2},{7,3},{8,12},{9,13},{10,... | collective-permute-start | bytes 393224 | tf_op jit(solution)/shard_map/ppermute | solution.py:386
  61.5 5.3 %copy-start = (s32[32]{0:T(128)S(1)}, s32[32]{0:T(128)}, u32[]{:S(2)}) copy-start(s32[32]{0:T(128)} %counts_ref.1) | copy-start | bytes 388
  61.5 53.6 %all-to-all-start.1 = ((f32[32,128,128]{2,1,0:T(8,128)}), f32[32,128,128]{2,1,0:T(8,128)S(1)}, u32[]{:S(2)}, u32[]{:S(2)}) async-start(f32[32,128,128]{2,1,0:T(8,128)} %analyse.1), calls=%async_computation.1 | async-start | bytes 4194304 | tf_op jit(solution)/shard_map/all_to_all | solution.py:465

commit v2 on v1

--- a/solution.py
+++ b/solution.py
@@ -28,7 +28,7 @@
     return lax.broadcasted_iota(jnp.int32, (ROWS, LANES), 0)
 
 
-def forecast_kernel(places_ref, noise_ref, x_ref, out_ref, mine_ref, rows_ref, state_ref, tile_ref, table_ref, scalar_ref, table_sem, in_sem, out_sem, *, members):
+def forecast_kernel(places_ref, noise_ref, x_ref, out_ref, mine_ref, rows_ref, state_ref, tile_ref, table_ref, scalar_ref, table_sem, out_sem, *, members):
     height = x_ref.shape[0]
     blocks = places_ref.shape[0]
     tiles = height // LANES
@@ -45,12 +45,8 @@
     def tile_rows(tile):
         return slice(tile * LANES, (tile + 1) * LANES)
 
-    incoming = [pltpu.make_async_copy(x_ref.at[tile_rows(tile)], rows_ref.at[tile_rows(tile)], in_sem.at[tile]) for tile in range(tiles)]
-    for copy in incoming:
-        copy.start()
-    for tile, copy in enumerate(incoming):
-        copy.wait()
-        tile_ref[tile * tile_pitch : tile * tile_pitch + LANES, :] = (rows_ref[tile_rows(tile), :] * TIME_STEP).T
+    for tile in range(tiles):
+        tile_ref[tile * tile_pitch : tile * tile_pitch + LANES, :] = (x_ref[tile_rows(tile), :] * TIME_STEP).T
     for cell in range(LANES):
         for half in range(halves):
             begin = cell * tiles + half * ROWS
@@ -107,10 +103,10 @@
         for half in range(halves):
             begin = cell * cell_pitch + half * ROWS
             tile_ref[begin : begin + ROWS, :] = group(cell)[half]
-    outgoing = [pltpu.make_async_copy(rows_ref.at[tile_rows(tile)], out_ref.at[tile_rows(tile)], out_sem.at[tile]) for tile in range(tiles)]
-    for tile, copy in enumerate(outgoing):
+    for tile in range(tiles):
         rows_ref[tile_rows(tile), :] = tile_ref[pl.ds(tile, LANES, stride=cell_pitch), :].T * (1.0 / TIME_STEP)
-        copy.start()
+    out_copy = pltpu.make_async_copy(rows_ref, out_ref, out_sem)
+    out_copy.start()
     table_copy.wait()
 
     def gather(block, carry):
@@ -133,8 +129,7 @@
     for block in range(blocks):
         begin = (blocks + block) * members
         mine_ref[begin : begin + members, :] = noise_ref[:, block * LANES : (block + 1) * LANES]
-    for copy in outgoing:
-        copy.wait()
+    out_copy.wait()
 
 
 def dot(a, b, contract, precision=HIGH):
@@ -269,7 +264,11 @@
         innovations.append(picked[total:])
         anomaly = equivalents - jnp.sum(equivalents, axis=0, keepdims=True) * (1.0 / total)
         anomalies.append(anomaly)
-        covariance = dot(anomaly.T, anomaly, ((1,), (0,))) * (1.0 / (total - 1))
+        high, middle, low = split_three(anomaly.T)
+        left = jnp.concatenate([high, high, middle, high, low, middle], axis=1)
+        high, middle, low = split_three(anomaly)
+        right = jnp.concatenate([high, middle, high, low, high, middle], axis=0)
+        covariance = dot(left, right, ((1,), (0,)), lax.Precision.DEFAULT) * (1.0 / (total - 1))
         matrix_refs[region][...] = jnp.where(diagonal, covariance + errors_ref[region : region + 1, :], covariance)
     invert_all(matrix_refs, left_refs, right_refs, done_refs)
     for region in range(regions):
@@ -389,10 +388,7 @@
 
     pick, errors = pl.pallas_call(
         functools.partial(prepare_kernel, cells=float(cells), zone_cells=zone_cells),
-        out_shape=(
-            jax.ShapeDtypeStruct((regions, observations, local), jnp.bfloat16),
-            jax.ShapeDtypeStruct((regions, local), jnp.float32),
-        ),
+        out_shape=(pltpu.VMEM((regions, observations, local), jnp.bfloat16), pltpu.VMEM((regions, local), jnp.float32)),
         in_specs=[whole(pltpu.SMEM), whole(), whole(), whole()],
         out_specs=(whole(),) * 2,
         name="prepare",
@@ -407,7 +403,7 @@
             jax.ShapeDtypeStruct((height, LANES), jnp.float32),
             jax.ShapeDtypeStruct((2 * blocks * members, LANES), jnp.float32),
         ),
-        in_specs=[whole(), whole(), whole(pltpu.HBM)],
+        in_specs=[whole()] * 3,
         out_specs=(whole(pltpu.HBM), whole()),
         scratch_shapes=[
             pltpu.VMEM((height, LANES), jnp.float32),
@@ -416,8 +412,7 @@
             pltpu.VMEM((2 * blocks, LANES), jnp.int32),
             pltpu.SMEM((2 * blocks, LANES), jnp.int32),
             pltpu.SemaphoreType.DMA,
-            pltpu.SemaphoreType.DMA((tiles,)),
-            pltpu.SemaphoreType.DMA((tiles,)),
+            pltpu.SemaphoreType.DMA,
         ],
         name="forecast",
     )(measured_indexes.reshape(blocks, LANES), perturbation, runs)
@@ -428,7 +423,6 @@
     far = []
     for mask in far_masks:
         far.append(swap(near, mask[0]))
-    state, near = lax.optimization_barrier((state, near))
     own_cells = exchange(state.reshape(devices, height // devices, LANES))
     partner = swap(near, depth)
     partners = swap(jnp.concatenate(far), depth)
@@ -438,7 +432,7 @@
     place = in_vmem if sum(piece.size for piece in pieces) * 4 <= VMEM_PIECES else lambda value: value
     transform = pl.pallas_call(
         functools.partial(solve_kernel, masks=masks),
-        out_shape=jax.ShapeDtypeStruct((regions, total, total), jnp.float32),
+        out_shape=pltpu.VMEM((regions, total, total), jnp.float32),
         in_specs=[whole(pltpu.SMEM)] + [whole()] * (4 + len(pieces)),
         out_specs=whole(),
         scratch_shapes=[
@@ -447,7 +441,7 @@
             *invert_scratch(regions, local),
         ],
         name="solve",
-    )(me, pick, errors, values, variance, *map(place, pieces))
+    )(me, place(pick), place(errors), values, variance, *map(place, pieces))
 
     outgoing = pl.pallas_call(
         apply_kernel,
@@ -461,7 +455,7 @@
             pltpu.SemaphoreType.DMA((4,)),
         ],
         name="analyse",
-    )(counts, transform, in_vmem(own_cells))
+    )(counts, in_vmem(transform), in_vmem(own_cells))
     owned = exchange(outgoing)
 
     chunks = 8

time: 119 us -> 125 us (1.050)
  waiting for transfers between devices: 65.1 us -> 78 us
  Pallas kernels: 32.1 us -> 27.7 us
  starting transfers between devices: 20.1 us -> 18 us
    ppermute x8, waiting for transfers between devices: 17.4 us -> 30.4 us  [swap(): lax.ppermute(value, AXES, [(device, device ^ bits) for device in range(de...]
    all_to_all x1, starting transfers between devices: 5.25 us -> 3.25 us  [per_device(): owned = exchange(outgoing)]
    pallas_call x1, Pallas kernels: 11.2 us -> 9.28 us  [per_device(): pl.pallas_call(functools.partial(forecast_kernel, members=members), out_s...]
    pallas_call x1, Pallas kernels: 11.9 us -> 10.6 us  [per_device(): pl.pallas_call(functools.partial(solve_kernel, masks=masks), out_shape=pl...]
  transfers between devices with their start and end apart: 10 -> 10, of which waited for: 5 -> 6; matrix products, arithmetic and copies ran while one was open for 1% -> 1% of each run, Pallas kernels for 12% -> 10%
where the time goes in v2:
time: 125 us
  waiting for transfers between devices  78 us (62%)
  Pallas kernels  27.7 us (22%)
  starting transfers between devices  18 us (14%)
    all_to_all x1, waiting for transfers between devices, per_device(): owned = exchange(outgoing)  47.7 us
    ppermute x8, waiting for transfers between devices, swap(): lax.ppermute(value, AXES, [(device, device ^ bits) for device in range(de...  30.4 us
    pallas_call x1, Pallas kernels, per_device(): pl.pallas_call(functools.partial(solve_kernel, masks=masks), out_shape=pl...  10.6 us
    pallas_call x1, Pallas kernels, per_device(): pl.pallas_call(functools.partial(forecast_kernel, members=members), out_s...  9.28 us
    ppermute x8, starting transfers between devices, swap(): lax.ppermute(value, AXES, [(device, device ^ bits) for device in range(de...  7.69 us
    all_to_all x1, starting transfers between devices, per_device(): own_cells = exchange(state.reshape(devices, height // devices, LANES))  7.09 us
    pallas_call x1, Pallas kernels, per_device(): pl.pallas_call(advance_kernel, out_shape=jax.ShapeDtypeStruct((CAP, cells...  3.64 us
    all_to_all x1, starting transfers between devices, per_device(): owned = exchange(outgoing)  3.25 us
  transfers between devices with their start and end apart: 10, of which 6 were waited for; matrix products, arithmetic and copies ran while one was open for 1% of the time, Pallas kernels for 10%

profile of v2, /device:TPU:1, one launch (start us, length us, event | category | flops | bytes accessed | tf_op | source)
XLA Modules:
  0.0 124.6 jit_solution(3876384916830978212)
XLA Ops:
  0.0 9.3 %forecast.1 = (f32[2048,128]{1,0:T(8,128)}, f32[64,128]{1,0:T(8,128)}) custom-call(s32[8,128]{1,0:T(8,128)} %bitcast.18, f32[4,1024]{1,0:T(4,128)} %noise_ref.1, f32[2048,128]{1,0:T(8,128)} %bitcast.12), custom_call_target="tpu_custom_call" | custom-call | tf_op jit(solution)/shard_map/forecast/pallas_call | solution.py:400
  9.3 7.1 %all-to-all-start = ((f32[32,64,128]{2,1,0:T(8,128)}), f32[32,64,128]{2,1,0:T(8,128)S(1)}, u32[]{:S(2)}, u32[]{:S(2)}) async-start(f32[32,64,128]{2,1,0:T(8,128)} %bitcast.13), calls=%async_computation | async-start | bytes 2097152 | tf_op jit(solution)/shard_map/all_to_all | solution.py:426
  16.4 3.3 %collective-permute-start.2 = (f32[1,64,128]{2,1,0:T(8,128)S(1)}, f32[1,64,128]{2,1,0:T(8,128)S(1)}, u32[]{:S(2)}, u32[]{:S(2)}) collective-permute-start(f32[1,64,128]{2,1,0:T(8,128)S(1)} %bitcast.14), channel_id=1, source_target_pairs={{0,3},{1,2},{2,1},{3,0},{4,7},{5,6},{6,5},{7,4},{8,11},{9,10},{10,... | collective-permute-start | bytes 98312 | tf_op jit(solution)/shard_map/ppermute | solution.py:385
  19.7 0.0 collective-permute-start.1
  19.7 0.4 collective-permute-start
  20.0 17.9 %collective-permute-done.2 = f32[1,64,128]{2,1,0:T(8,128)S(1)} collective-permute-done((f32[1,64,128]{2,1,0:T(8,128)S(1)}, f32[1,64,128]{2,1,0:T(8,128)S(1)}, u32[]{:S(2)}, u32[]{:S(2)}) %collective-permute-start.2) | collective-permute-done | bytes 32800 | tf_op jit(solution)/shard_map/ppermute | solution.py:385
  37.9 6.5 %collective-permute-done.1 = f32[1,64,128]{2,1,0:T(8,128)S(1)} collective-permute-done((f32[1,64,128]{2,1,0:T(8,128)S(1)}, f32[1,64,128]{2,1,0:T(8,128)S(1)}, u32[]{:S(2)}, u32[]{:S(2)}) %collective-permute-start.1) | collective-permute-done | bytes 32800 | tf_op jit(solution)/shard_map/ppermute | solution.py:385
  44.4 2.2 %collective-permute-start.6 = (f32[4,64,128]{2,1,0:T(8,128)S(1)}, f32[4,64,128]{2,1,0:T(8,128)S(1)}, u32[]{:S(2)}, u32[]{:S(2)}) collective-permute-start(f32[4,64,128]{2,1,0:T(8,128)S(1)} %pad_maximum_fusion.1.refs_0_), channel_id=1, source_target_pairs={{0,24},{1,25},{2,26},{3,27},{4,28},{5,29},{6,30},{7,31},{8,16},{9,... | collective-permute-start | bytes 393224 | tf_op jit(solution)/shard_map/ppermute | solution.py:385
  46.6 0.2 collective-permute-start.5
  46.9 0.3 collective-permute-start.4
  47.1 2.1 %collective-permute-done.6.refs_4_ = f32[4,64,128]{2,1,0:T(8,128)S(1)} collective-permute-done((f32[4,64,128]{2,1,0:T(8,128)S(1)}, f32[4,64,128]{2,1,0:T(8,128)S(1)}, u32[]{:S(2)}, u32[]{:S(2)}) %collective-permute-start.6) | collective-permute-done | bytes 131104 | tf_op jit(solution)/shard_map/ppermute | solution.py:385
  49.2 3.8 %collective-permute-done.5.refs_3_ = f32[4,64,128]{2,1,0:T(8,128)S(1)} collective-permute-done((f32[4,64,128]{2,1,0:T(8,128)S(1)}, f32[4,64,128]{2,1,0:T(8,128)S(1)}, u32[]{:S(2)}, u32[]{:S(2)}) %collective-permute-start.5) | collective-permute-done | bytes 131104 | tf_op jit(solution)/shard_map/ppermute | solution.py:385
  53.0 0.0 collective-permute-done.4.refs_2_
  53.0 1.3 %collective-permute-start.7 = (f32[12,64,128]{2,1,0:T(8,128)S(1)}, f32[12,64,128]{2,1,0:T(8,128)S(1)}, u32[]{:S(2)}, u32[]{:S(2)}) collective-permute-start(f32[12,64,128]{2,1,0:T(8,128)S(1)} %pad_maximum_fusion), channel_id=1, source_target_pairs={{0,4},{1,5},{2,6},{3,7},{4,0},{5,1},{6,2},{7,3},{8,12},{9,13},{10,... | collective-permute-start | bytes 1179656 | tf_op jit(solution)/shard_map/ppermute | solution.py:385
  54.3 0.1 collective-permute-start.3
  54.3 1.3 %prepare.1 = (bf16[4,1024,128]{2,1,0:T(8,128)(2,1)S(1)}, f32[4,128]{1,0:T(4,128)S(1)}) custom-call(s32[1]{0:T(128)S(6)} %mul.7.zone_ref, s32[128,128]{1,0:T(8,128)} %neighbours_ref.1, f32[1,1024]{1,0:T(1,128)} %bitcast.20, s32[1,1024]{1,0:T(1,128)} %bitcast.19), custom_call_target="tpu_custom_call" | custom-call | tf_op jit(solution)/shard_map/prepare/pallas_call | solution.py:389
  55.6 0.2 collective-permute-done.3.refs_1_
  55.8 10.6 %solve.1.transform_ref = f32[4,128,128]{2,1,0:T(8,128)S(1)} custom-call(s32[1]{0:T(128)} %bitcast.me_ref, bf16[4,1024,128]{2,1,0:T(8,128)(2,1)S(1)} %get-tuple-element.9.pick_ref, f32[4,128]{1,0:T(4,128)S(1)} %get-tuple-element.10.errors_ref, f32[1,1024]{1,0:T(1,128)} %bitcast.22, f32[1,1024]{1,0:T(1,128)} %bitcast.21, ...), custom_call_target="tpu_custom_call" | custom-call | tf_op jit(solution)/shard_map/solve/pallas_call | solution.py:433
  66.5 2.9 %analyse.1 = f32[32,128,128]{2,1,0:T(8,128)} custom-call(s32[32]{0:T(128)} %counts_ref.1, f32[4,128,128]{2,1,0:T(8,128)S(1)} %solve.1.transform_ref, f32[32,64,128]{2,1,0:T(8,128)S(1)} %all-to-all-done.cells_ref), custom_call_target="tpu_custom_call" | custom-call | tf_op jit(solution)/shard_map/analyse/pallas_call | solution.py:446
  69.3 0.0 copy-start.1
  69.3 3.2 %all-to-all-start.1 = ((f32[32,128,128]{2,1,0:T(8,128)}), f32[32,128,128]{2,1,0:T(8,128)S(1)}, u32[]{:S(2)}, u32[]{:S(2)}) async-start(f32[32,128,128]{2,1,0:T(8,128)} %analyse.1), calls=%async_computation.1 | async-start | bytes 4194304 | tf_op jit(solution)/shard_map/all_to_all | solution.py:459
  72.6 0.7 dynamic_slice.3.count_ref
  73.3 47.7 %all-to-all-done.1.rows_ref = f32[32,128,128]{2,1,0:T(8,128)S(1)} async-done(((f32[32,128,128]{2,1,0:T(8,128)}), f32[32,128,128]{2,1,0:T(8,128)S(1)}, u32[]{:S(2)}, u32[]{:S(2)}) %all-to-all-start.1) | async-done | bytes 2097184 | tf_op jit(solution)/shard_map/all_to_all | solution.py:459
  120.9 3.6 %advance.1 = f32[8,65536]{1,0:T(8,128)} custom-call(s32[1]{0:T(128)} %dynamic_slice.3.count_ref, f32[32,128,128]{2,1,0:T(8,128)S(1)} %all-to-all-done.1.rows_ref), custom_call_target="tpu_custom_call" | custom-call | tf_op jit(solution)/shard_map/advance/pallas_call | solution.py:462
  (8 shorter events, 0.1 us)
Async XLA Ops:
  9.3 7.1 %copy-start = (f32[64,128]{1,0:T(8,128)S(1)}, f32[64,128]{1,0:T(8,128)}, u32[]{:S(2)}) copy-start(f32[64,128]{1,0:T(8,128)} %get-tuple-element.11) | copy-start | bytes 98308
  9.3 57.2 %all-to-all-start = ((f32[32,64,128]{2,1,0:T(8,128)}), f32[32,64,128]{2,1,0:T(8,128)S(1)}, u32[]{:S(2)}, u32[]{:S(2)}) async-start(f32[32,64,128]{2,1,0:T(8,128)} %bitcast.13), calls=%async_computation | async-start | bytes 2097152 | tf_op jit(solution)/shard_map/all_to_all | solution.py:426
  16.4 21.5 %collective-permute-start.2 = (f32[1,64,128]{2,1,0:T(8,128)S(1)}, f32[1,64,128]{2,1,0:T(8,128)S(1)}, u32[]{:S(2)}, u32[]{:S(2)}) collective-permute-start(f32[1,64,128]{2,1,0:T(8,128)S(1)} %bitcast.14), channel_id=1, source_target_pairs={{0,3},{1,2},{2,1},{3,0},{4,7},{5,6},{6,5},{7,4},{8,11},{9,10},{10,... | collective-permute-start | bytes 98312 | tf_op jit(solution)/shard_map/ppermute | solution.py:385
  19.7 24.7 %collective-permute-start.1 = (f32[1,64,128]{2,1,0:T(8,128)S(1)}, f32[1,64,128]{2,1,0:T(8,128)S(1)}, u32[]{:S(2)}, u32[]{:S(2)}) collective-permute-start(f32[1,64,128]{2,1,0:T(8,128)S(1)} %bitcast.15), channel_id=1, source_target_pairs={{0,2},{1,3},{2,0},{3,1},{4,6},{5,7},{6,4},{7,5},{8,10},{9,11},{10,... | collective-permute-start | bytes 98312 | tf_op jit(solution)/shard_map/ppermute | solution.py:385
  19.7 24.7 %collective-permute-start = (f32[1,64,128]{2,1,0:T(8,128)S(1)}, f32[1,64,128]{2,1,0:T(8,128)S(1)}, u32[]{:S(2)}, u32[]{:S(2)}) collective-permute-start(f32[1,64,128]{2,1,0:T(8,128)S(1)} %bitcast.16), channel_id=1, source_target_pairs={{0,1},{1,0},{2,3},{3,2},{4,5},{5,4},{6,7},{7,6},{8,9},{9,8},{10,11... | collective-permute-start | bytes 98312 | tf_op jit(solution)/shard_map/ppermute | solution.py:385
  44.4 4.8 %collective-permute-start.6 = (f32[4,64,128]{2,1,0:T(8,128)S(1)}, f32[4,64,128]{2,1,0:T(8,128)S(1)}, u32[]{:S(2)}, u32[]{:S(2)}) collective-permute-start(f32[4,64,128]{2,1,0:T(8,128)S(1)} %pad_maximum_fusion.1.refs_0_), channel_id=1, source_target_pairs={{0,24},{1,25},{2,26},{3,27},{4,28},{5,29},{6,30},{7,31},{8,16},{9,... | collective-permute-start | bytes 393224 | tf_op jit(solution)/shard_map/ppermute | solution.py:385
  46.6 6.4 %collective-permute-start.5 = (f32[4,64,128]{2,1,0:T(8,128)S(1)}, f32[4,64,128]{2,1,0:T(8,128)S(1)}, u32[]{:S(2)}, u32[]{:S(2)}) collective-permute-start(f32[4,64,128]{2,1,0:T(8,128)S(1)} %pad_maximum_fusion.1.refs_0_), channel_id=1, source_target_pairs={{0,16},{1,17},{2,18},{3,19},{4,20},{5,21},{6,22},{7,23},{8,24},{9,... | collective-permute-start | bytes 393224 | tf_op jit(solution)/shard_map/ppermute | solution.py:385
  46.9 6.1 %collective-permute-start.4 = (f32[4,64,128]{2,1,0:T(8,128)S(1)}, f32[4,64,128]{2,1,0:T(8,128)S(1)}, u32[]{:S(2)}, u32[]{:S(2)}) collective-permute-start(f32[4,64,128]{2,1,0:T(8,128)S(1)} %pad_maximum_fusion.1.refs_0_), channel_id=1, source_target_pairs={{0,8},{1,9},{2,10},{3,11},{4,12},{5,13},{6,14},{7,15},{8,0},{9,1},... | collective-permute-start | bytes 393224 | tf_op jit(solution)/shard_map/ppermute | solution.py:385
  53.0 2.8 %collective-permute-start.7 = (f32[12,64,128]{2,1,0:T(8,128)S(1)}, f32[12,64,128]{2,1,0:T(8,128)S(1)}, u32[]{:S(2)}, u32[]{:S(2)}) collective-permute-start(f32[12,64,128]{2,1,0:T(8,128)S(1)} %pad_maximum_fusion), channel_id=1, source_target_pairs={{0,4},{1,5},{2,6},{3,7},{4,0},{5,1},{6,2},{7,3},{8,12},{9,13},{10,... | collective-permute-start | bytes 1179656 | tf_op jit(solution)/shard_map/ppermute | solution.py:385
  54.3 1.5 %collective-permute-start.3 = (f32[4,64,128]{2,1,0:T(8,128)S(1)}, f32[4,64,128]{2,1,0:T(8,128)S(1)}, u32[]{:S(2)}, u32[]{:S(2)}) collective-permute-start(f32[4,64,128]{2,1,0:T(8,128)S(1)} %pad_maximum_fusion.1.refs_0_), channel_id=1, source_target_pairs={{0,4},{1,5},{2,6},{3,7},{4,0},{5,1},{6,2},{7,3},{8,12},{9,13},{10,... | collective-permute-start | bytes 393224 | tf_op jit(solution)/shard_map/ppermute | solution.py:385
  69.3 3.3 %copy-start.1 = (s32[32]{0:T(128)S(1)}, s32[32]{0:T(128)}, u32[]{:S(2)}) copy-start(s32[32]{0:T(128)} %counts_ref.1) | copy-start | bytes 388
  69.3 51.6 %all-to-all-start.1 = ((f32[32,128,128]{2,1,0:T(8,128)}), f32[32,128,128]{2,1,0:T(8,128)S(1)}, u32[]{:S(2)}, u32[]{:S(2)}) async-start(f32[32,128,128]{2,1,0:T(8,128)} %analyse.1), calls=%async_computation.1 | async-start | bytes 4194304 | tf_op jit(solution)/shard_map/all_to_all | solution.py:459

commit v3 on v2

--- a/solution.py
+++ b/solution.py
@@ -109,7 +109,7 @@
     out_copy.start()
     table_copy.wait()
 
-    def gather(block, carry):
+    for block in range(blocks):
         picked = [jnp.zeros((ROWS, LANES), jnp.float32) for _ in range(4)]
         for number in range(LANES):
             begin = pl.multiple_of(scalar_ref[block, number], ROWS)
@@ -118,14 +118,11 @@
         both = picked[0]
         for number in range(1, 4):
             both = jnp.where(lane % 4 == number, picked[number], both)
-        part_of = (places_ref[pl.ds(block, 1), :] // LANES) % parts
+        part_of = (places_ref[block : block + 1, :] // LANES) % parts
         chosen = both
         for part in range(1, parts):
             chosen = jnp.where(part_of == part, pltpu.roll(both, ROWS - part * members, axis=0), chosen)
-        mine_ref[pl.ds(block * members, members), :] = chosen[:members]
-        return carry
-
-    lax.fori_loop(0, blocks, gather, 0)
+        mine_ref[block * members : (block + 1) * members, :] = chosen[:members]
     for block in range(blocks):
         begin = (blocks + block) * members
         mine_ref[begin : begin + members, :] = noise_ref[:, block * LANES : (block + 1) * LANES]
@@ -305,7 +302,7 @@
     offset = jnp.int32(0)
     copies = []
     for number in range(groups):
-        offset = lax.fori_loop(number * group, (number + 1) * group, window, offset)
+        offset = lax.fori_loop(number * group, (number + 1) * group, window, offset, unroll=True)
         span = slice(number * group, (number + 1) * group)
         copies.append(pltpu.make_async_copy(staging_ref.at[span], owned_ref.at[span], out_sem.at[number]))
         copies[-1].start()
@@ -458,7 +455,7 @@
     )(counts, in_vmem(transform), in_vmem(own_cells))
     owned = exchange(outgoing)
 
-    chunks = 8
+    chunks = 4
     return pl.pallas_call(
         advance_kernel,
         out_shape=jax.ShapeDtypeStruct((CAP, cells), jnp.float32),

time: 125 us -> 124 us (level)
  Pallas kernels: 27.7 us -> 26.4 us
where the time goes in v3:
time: 124 us; the launch traced here: 123 us
  waiting for transfers between devices  78 us (63%)
  Pallas kernels  26.4 us (21%)
  starting transfers between devices  18 us (15%)
    all_to_all x1, waiting for transfers between devices, per_device(): owned = exchange(outgoing)  47.7 us
    ppermute x8, waiting for transfers between devices, swap(): lax.ppermute(value, AXES, [(device, device ^ bits) for device in range(de...  30.4 us
    pallas_call x1, Pallas kernels, per_device(): pl.pallas_call(functools.partial(solve_kernel, masks=masks), out_shape=pl...  10.6 us
    pallas_call x1, Pallas kernels, per_device(): pl.pallas_call(functools.partial(forecast_kernel, members=members), out_s...  8.3 us
    ppermute x8, starting transfers between devices, swap(): lax.ppermute(value, AXES, [(device, device ^ bits) for device in range(de...  7.69 us
    all_to_all x1, starting transfers between devices, per_device(): own_cells = exchange(state.reshape(devices, height // devices, LANES))  7.09 us
    pallas_call x1, Pallas kernels, per_device(): pl.pallas_call(advance_kernel, out_shape=jax.ShapeDtypeStruct((CAP, cells...  3.38 us
    all_to_all x1, starting transfers between devices, per_device(): owned = exchange(outgoing)  3.25 us
  transfers between devices with their start and end apart: 10, of which 6 were waited for; matrix products, arithmetic and copies ran while one was open for 1% of the time, Pallas kernels for 10%

profile of v3, /device:TPU:1, one launch (start us, length us, event | category | flops | bytes accessed | tf_op | source)
XLA Modules:
  0.0 123.3 jit_solution(14265145494845403833)
XLA Ops:
  0.0 8.3 %forecast.1 = (f32[2048,128]{1,0:T(8,128)}, f32[64,128]{1,0:T(8,128)}) custom-call(s32[8,128]{1,0:T(8,128)} %bitcast.18, f32[4,1024]{1,0:T(4,128)} %noise_ref.1, f32[2048,128]{1,0:T(8,128)} %bitcast.12), custom_call_target="tpu_custom_call" | custom-call | tf_op jit(solution)/shard_map/forecast/pallas_call | solution.py:397
  8.3 7.1 %all-to-all-start = ((f32[32,64,128]{2,1,0:T(8,128)}), f32[32,64,128]{2,1,0:T(8,128)S(1)}, u32[]{:S(2)}, u32[]{:S(2)}) async-start(f32[32,64,128]{2,1,0:T(8,128)} %bitcast.13), calls=%async_computation | async-start | bytes 2097152 | tf_op jit(solution)/shard_map/all_to_all | solution.py:423
  15.4 3.3 %collective-permute-start.2 = (f32[1,64,128]{2,1,0:T(8,128)S(1)}, f32[1,64,128]{2,1,0:T(8,128)S(1)}, u32[]{:S(2)}, u32[]{:S(2)}) collective-permute-start(f32[1,64,128]{2,1,0:T(8,128)S(1)} %bitcast.14), channel_id=1, source_target_pairs={{0,3},{1,2},{2,1},{3,0},{4,7},{5,6},{6,5},{7,4},{8,11},{9,10},{10,... | collective-permute-start | bytes 98312 | tf_op jit(solution)/shard_map/ppermute | solution.py:382
  18.7 0.0 collective-permute-start.1
  18.7 0.4 collective-permute-start
  19.1 17.9 %collective-permute-done.2 = f32[1,64,128]{2,1,0:T(8,128)S(1)} collective-permute-done((f32[1,64,128]{2,1,0:T(8,128)S(1)}, f32[1,64,128]{2,1,0:T(8,128)S(1)}, u32[]{:S(2)}, u32[]{:S(2)}) %collective-permute-start.2) | collective-permute-done | bytes 32800 | tf_op jit(solution)/shard_map/ppermute | solution.py:382
  36.9 6.5 %collective-permute-done.1 = f32[1,64,128]{2,1,0:T(8,128)S(1)} collective-permute-done((f32[1,64,128]{2,1,0:T(8,128)S(1)}, f32[1,64,128]{2,1,0:T(8,128)S(1)}, u32[]{:S(2)}, u32[]{:S(2)}) %collective-permute-start.1) | collective-permute-done | bytes 32800 | tf_op jit(solution)/shard_map/ppermute | solution.py:382
  43.4 2.2 %collective-permute-start.6 = (f32[4,64,128]{2,1,0:T(8,128)S(1)}, f32[4,64,128]{2,1,0:T(8,128)S(1)}, u32[]{:S(2)}, u32[]{:S(2)}) collective-permute-start(f32[4,64,128]{2,1,0:T(8,128)S(1)} %pad_maximum_fusion.1.refs_0_), channel_id=1, source_target_pairs={{0,24},{1,25},{2,26},{3,27},{4,28},{5,29},{6,30},{7,31},{8,16},{9,... | collective-permute-start | bytes 393224 | tf_op jit(solution)/shard_map/ppermute | solution.py:382
  45.6 0.2 collective-permute-start.5
  45.9 0.3 collective-permute-start.4
  46.2 2.1 %collective-permute-done.6.refs_4_ = f32[4,64,128]{2,1,0:T(8,128)S(1)} collective-permute-done((f32[4,64,128]{2,1,0:T(8,128)S(1)}, f32[4,64,128]{2,1,0:T(8,128)S(1)}, u32[]{:S(2)}, u32[]{:S(2)}) %collective-permute-start.6) | collective-permute-done | bytes 131104 | tf_op jit(solution)/shard_map/ppermute | solution.py:382
  48.2 3.8 %collective-permute-done.5.refs_3_ = f32[4,64,128]{2,1,0:T(8,128)S(1)} collective-permute-done((f32[4,64,128]{2,1,0:T(8,128)S(1)}, f32[4,64,128]{2,1,0:T(8,128)S(1)}, u32[]{:S(2)}, u32[]{:S(2)}) %collective-permute-start.5) | collective-permute-done | bytes 131104 | tf_op jit(solution)/shard_map/ppermute | solution.py:382
  52.0 0.0 collective-permute-done.4.refs_2_
  52.0 1.3 %collective-permute-start.7 = (f32[12,64,128]{2,1,0:T(8,128)S(1)}, f32[12,64,128]{2,1,0:T(8,128)S(1)}, u32[]{:S(2)}, u32[]{:S(2)}) collective-permute-start(f32[12,64,128]{2,1,0:T(8,128)S(1)} %pad_maximum_fusion), channel_id=1, source_target_pairs={{0,4},{1,5},{2,6},{3,7},{4,0},{5,1},{6,2},{7,3},{8,12},{9,13},{10,... | collective-permute-start | bytes 1179656 | tf_op jit(solution)/shard_map/ppermute | solution.py:382
  53.3 0.1 collective-permute-start.3
  53.4 1.3 %prepare.1 = (bf16[4,1024,128]{2,1,0:T(8,128)(2,1)S(1)}, f32[4,128]{1,0:T(4,128)S(1)}) custom-call(s32[1]{0:T(128)S(6)} %mul.7.zone_ref, s32[128,128]{1,0:T(8,128)} %neighbours_ref.1, f32[1,1024]{1,0:T(1,128)} %bitcast.20, s32[1,1024]{1,0:T(1,128)} %bitcast.19), custom_call_target="tpu_custom_call" | custom-call | tf_op jit(solution)/shard_map/prepare/pallas_call | solution.py:386
  54.6 0.2 collective-permute-done.3.refs_1_
  54.8 10.6 %solve.1.transform_ref = f32[4,128,128]{2,1,0:T(8,128)S(1)} custom-call(s32[1]{0:T(128)} %bitcast.me_ref, bf16[4,1024,128]{2,1,0:T(8,128)(2,1)S(1)} %get-tuple-element.9.pick_ref, f32[4,128]{1,0:T(4,128)S(1)} %get-tuple-element.10.errors_ref, f32[1,1024]{1,0:T(1,128)} %bitcast.22, f32[1,1024]{1,0:T(1,128)} %bitcast.21, ...), custom_call_target="tpu_custom_call" | custom-call | tf_op jit(solution)/shard_map/solve/pallas_call | solution.py:430
  65.5 2.8 %analyse.1 = f32[32,128,128]{2,1,0:T(8,128)} custom-call(s32[32]{0:T(128)} %counts_ref.1, f32[4,128,128]{2,1,0:T(8,128)S(1)} %solve.1.transform_ref, f32[32,64,128]{2,1,0:T(8,128)S(1)} %all-to-all-done.cells_ref), custom_call_target="tpu_custom_call" | custom-call | tf_op jit(solution)/shard_map/analyse/pallas_call | solution.py:443
  68.3 0.0 copy-start.1
  68.3 3.3 %all-to-all-start.1 = ((f32[32,128,128]{2,1,0:T(8,128)}), f32[32,128,128]{2,1,0:T(8,128)S(1)}, u32[]{:S(2)}, u32[]{:S(2)}) async-start(f32[32,128,128]{2,1,0:T(8,128)} %analyse.1), calls=%async_computation.1 | async-start | bytes 4194304 | tf_op jit(solution)/shard_map/all_to_all | solution.py:456
  71.6 0.7 dynamic_slice.3.count_ref
  72.3 47.7 %all-to-all-done.1.rows_ref = f32[32,128,128]{2,1,0:T(8,128)S(1)} async-done(((f32[32,128,128]{2,1,0:T(8,128)}), f32[32,128,128]{2,1,0:T(8,128)S(1)}, u32[]{:S(2)}, u32[]{:S(2)}) %all-to-all-start.1) | async-done | bytes 2097184 | tf_op jit(solution)/shard_map/all_to_all | solution.py:456
  119.9 3.4 %advance.1 = f32[8,65536]{1,0:T(8,128)} custom-call(s32[1]{0:T(128)} %dynamic_slice.3.count_ref, f32[32,128,128]{2,1,0:T(8,128)S(1)} %all-to-all-done.1.rows_ref), custom_call_target="tpu_custom_call" | custom-call | tf_op jit(solution)/shard_map/advance/pallas_call | solution.py:459
  (8 shorter events, 0.1 us)
Async XLA Ops:
  8.3 7.1 %copy-start = (f32[64,128]{1,0:T(8,128)S(1)}, f32[64,128]{1,0:T(8,128)}, u32[]{:S(2)}) copy-start(f32[64,128]{1,0:T(8,128)} %get-tuple-element.11) | copy-start | bytes 98308
  8.3 57.2 %all-to-all-start = ((f32[32,64,128]{2,1,0:T(8,128)}), f32[32,64,128]{2,1,0:T(8,128)S(1)}, u32[]{:S(2)}, u32[]{:S(2)}) async-start(f32[32,64,128]{2,1,0:T(8,128)} %bitcast.13), calls=%async_computation | async-start | bytes 2097152 | tf_op jit(solution)/shard_map/all_to_all | solution.py:423
  15.4 21.5 %collective-permute-start.2 = (f32[1,64,128]{2,1,0:T(8,128)S(1)}, f32[1,64,128]{2,1,0:T(8,128)S(1)}, u32[]{:S(2)}, u32[]{:S(2)}) collective-permute-start(f32[1,64,128]{2,1,0:T(8,128)S(1)} %bitcast.14), channel_id=1, source_target_pairs={{0,3},{1,2},{2,1},{3,0},{4,7},{5,6},{6,5},{7,4},{8,11},{9,10},{10,... | collective-permute-start | bytes 98312 | tf_op jit(solution)/shard_map/ppermute | solution.py:382
  18.7 24.7 %collective-permute-start.1 = (f32[1,64,128]{2,1,0:T(8,128)S(1)}, f32[1,64,128]{2,1,0:T(8,128)S(1)}, u32[]{:S(2)}, u32[]{:S(2)}) collective-permute-start(f32[1,64,128]{2,1,0:T(8,128)S(1)} %bitcast.15), channel_id=1, source_target_pairs={{0,2},{1,3},{2,0},{3,1},{4,6},{5,7},{6,4},{7,5},{8,10},{9,11},{10,... | collective-permute-start | bytes 98312 | tf_op jit(solution)/shard_map/ppermute | solution.py:382
  18.7 24.7 %collective-permute-start = (f32[1,64,128]{2,1,0:T(8,128)S(1)}, f32[1,64,128]{2,1,0:T(8,128)S(1)}, u32[]{:S(2)}, u32[]{:S(2)}) collective-permute-start(f32[1,64,128]{2,1,0:T(8,128)S(1)} %bitcast.16), channel_id=1, source_target_pairs={{0,1},{1,0},{2,3},{3,2},{4,5},{5,4},{6,7},{7,6},{8,9},{9,8},{10,11... | collective-permute-start | bytes 98312 | tf_op jit(solution)/shard_map/ppermute | solution.py:382
  43.4 4.8 %collective-permute-start.6 = (f32[4,64,128]{2,1,0:T(8,128)S(1)}, f32[4,64,128]{2,1,0:T(8,128)S(1)}, u32[]{:S(2)}, u32[]{:S(2)}) collective-permute-start(f32[4,64,128]{2,1,0:T(8,128)S(1)} %pad_maximum_fusion.1.refs_0_), channel_id=1, source_target_pairs={{0,24},{1,25},{2,26},{3,27},{4,28},{5,29},{6,30},{7,31},{8,16},{9,... | collective-permute-start | bytes 393224 | tf_op jit(solution)/shard_map/ppermute | solution.py:382
  45.6 6.4 %collective-permute-start.5 = (f32[4,64,128]{2,1,0:T(8,128)S(1)}, f32[4,64,128]{2,1,0:T(8,128)S(1)}, u32[]{:S(2)}, u32[]{:S(2)}) collective-permute-start(f32[4,64,128]{2,1,0:T(8,128)S(1)} %pad_maximum_fusion.1.refs_0_), channel_id=1, source_target_pairs={{0,16},{1,17},{2,18},{3,19},{4,20},{5,21},{6,22},{7,23},{8,24},{9,... | collective-permute-start | bytes 393224 | tf_op jit(solution)/shard_map/ppermute | solution.py:382
  45.9 6.1 %collective-permute-start.4 = (f32[4,64,128]{2,1,0:T(8,128)S(1)}, f32[4,64,128]{2,1,0:T(8,128)S(1)}, u32[]{:S(2)}, u32[]{:S(2)}) collective-permute-start(f32[4,64,128]{2,1,0:T(8,128)S(1)} %pad_maximum_fusion.1.refs_0_), channel_id=1, source_target_pairs={{0,8},{1,9},{2,10},{3,11},{4,12},{5,13},{6,14},{7,15},{8,0},{9,1},... | collective-permute-start | bytes 393224 | tf_op jit(solution)/shard_map/ppermute | solution.py:382
  52.0 2.8 %collective-permute-start.7 = (f32[12,64,128]{2,1,0:T(8,128)S(1)}, f32[12,64,128]{2,1,0:T(8,128)S(1)}, u32[]{:S(2)}, u32[]{:S(2)}) collective-permute-start(f32[12,64,128]{2,1,0:T(8,128)S(1)} %pad_maximum_fusion), channel_id=1, source_target_pairs={{0,4},{1,5},{2,6},{3,7},{4,0},{5,1},{6,2},{7,3},{8,12},{9,13},{10,... | collective-permute-start | bytes 1179656 | tf_op jit(solution)/shard_map/ppermute | solution.py:382
  53.3 1.5 %collective-permute-start.3 = (f32[4,64,128]{2,1,0:T(8,128)S(1)}, f32[4,64,128]{2,1,0:T(8,128)S(1)}, u32[]{:S(2)}, u32[]{:S(2)}) collective-permute-start(f32[4,64,128]{2,1,0:T(8,128)S(1)} %pad_maximum_fusion.1.refs_0_), channel_id=1, source_target_pairs={{0,4},{1,5},{2,6},{3,7},{4,0},{5,1},{6,2},{7,3},{8,12},{9,13},{10,... | collective-permute-start | bytes 393224 | tf_op jit(solution)/shard_map/ppermute | solution.py:382
  68.3 3.3 %copy-start.1 = (s32[32]{0:T(128)S(1)}, s32[32]{0:T(128)}, u32[]{:S(2)}) copy-start(s32[32]{0:T(128)} %counts_ref.1) | copy-start | bytes 388
  68.3 51.6 %all-to-all-start.1 = ((f32[32,128,128]{2,1,0:T(8,128)}), f32[32,128,128]{2,1,0:T(8,128)S(1)}, u32[]{:S(2)}, u32[]{:S(2)}) async-start(f32[32,128,128]{2,1,0:T(8,128)} %analyse.1), calls=%async_computation.1 | async-start | bytes 4194304 | tf_op jit(solution)/shard_map/all_to_all | solution.py:456

commit v4 on v3

--- a/solution.py
+++ b/solution.py
@@ -422,9 +422,9 @@
         far.append(swap(near, mask[0]))
     own_cells = exchange(state.reshape(devices, height // devices, LANES))
     partner = swap(near, depth)
-    partners = swap(jnp.concatenate(far), depth)
-    pieces = [near, partner, *far, partners]
-    masks = [near_mask, [depth ^ bits for bits in near_mask], *far_masks, [depth ^ bits for mask in far_masks for bits in mask]]
+    partners = [swap(value, depth) for value in far]
+    pieces = [near, partner, *far, *partners]
+    masks = [near_mask, [depth ^ bits for bits in near_mask], *far_masks, *[[depth ^ bits for bits in mask] for mask in far_masks]]
 
     place = in_vmem if sum(piece.size for piece in pieces) * 4 <= VMEM_PIECES else lambda value: value
     transform = pl.pallas_call(
@@ -449,7 +449,7 @@
             pltpu.VMEM((total, share_tiles * LANES), jnp.float32),
             pltpu.VMEM((share_tiles, total + ROWS, LANES), jnp.float32),
             pltpu.VMEM((devices, share_tiles * CAP, LANES), jnp.float32),
-            pltpu.SemaphoreType.DMA((4,)),
+            pltpu.SemaphoreType.DMA((8,)),
         ],
         name="analyse",
     )(counts, in_vmem(transform), in_vmem(own_cells))

time: 124 us -> 123 us (level)
  waiting for transfers between devices: 78 us -> 72.8 us
  starting transfers between devices: 18 us -> 23.2 us
    ppermute x8 -> x10, waiting for transfers between devices: 30.4 us -> 25 us  [swap(): lax.ppermute(value, AXES, [(device, device ^ bits) for device in range(de...]
    ppermute x8 -> x10, starting transfers between devices: 7.69 us -> 12.7 us  [swap(): lax.ppermute(value, AXES, [(device, device ^ bits) for device in range(de...]
  transfers between devices with their start and end apart: 10 -> 12, of which waited for: 6 -> 4; matrix products, arithmetic and copies ran while one was open for 1% -> 0% of each run, Pallas kernels for 10% -> 10%
where the time goes in v4:
time: 123 us
  waiting for transfers between devices  72.8 us (59%)
  Pallas kernels  26.4 us (21%)
  starting transfers between devices  23.2 us (19%)
    all_to_all x1, waiting for transfers between devices, per_device(): owned = exchange(outgoing)  47.7 us
    ppermute x10, waiting for transfers between devices, swap(): lax.ppermute(value, AXES, [(device, device ^ bits) for device in range(de...  25 us
    ppermute x10, starting transfers between devices, swap(): lax.ppermute(value, AXES, [(device, device ^ bits) for device in range(de...  12.7 us
    pallas_call x1, Pallas kernels, per_device(): pl.pallas_call(functools.partial(solve_kernel, masks=masks), out_shape=pl...  10.6 us
    pallas_call x1, Pallas kernels, per_device(): pl.pallas_call(functools.partial(forecast_kernel, members=members), out_s...  8.3 us
    all_to_all x1, starting transfers between devices, per_device(): own_cells = exchange(state.reshape(devices, height // devices, LANES))  7.09 us
    all_to_all x1, starting transfers between devices, per_device(): owned = exchange(outgoing)  3.39 us
    pallas_call x1, Pallas kernels, per_device(): pl.pallas_call(advance_kernel, out_shape=jax.ShapeDtypeStruct((CAP, cells...  3.31 us
  transfers between devices with their start and end apart: 12, of which 4 were waited for; matrix products, arithmetic and copies ran while one was open for 0% of the time, Pallas kernels for 10%

profile of v4, /device:TPU:1, one launch (start us, length us, event | category | flops | bytes accessed | tf_op | source)
XLA Modules:
  0.0 123.1 jit_solution(14734696653498152968)
XLA Ops:
  0.0 8.3 %forecast.1 = (f32[2048,128]{1,0:T(8,128)}, f32[64,128]{1,0:T(8,128)}) custom-call(s32[8,128]{1,0:T(8,128)} %bitcast.18, f32[4,1024]{1,0:T(4,128)} %noise_ref.1, f32[2048,128]{1,0:T(8,128)} %bitcast.12), custom_call_target="tpu_custom_call" | custom-call | tf_op jit(solution)/shard_map/forecast/pallas_call | solution.py:397
  8.3 7.1 %all-to-all-start = ((f32[32,64,128]{2,1,0:T(8,128)}), f32[32,64,128]{2,1,0:T(8,128)S(1)}, u32[]{:S(2)}, u32[]{:S(2)}) async-start(f32[32,64,128]{2,1,0:T(8,128)} %bitcast.13), calls=%async_computation | async-start | bytes 2097152 | tf_op jit(solution)/shard_map/all_to_all | solution.py:423
  15.4 3.3 %collective-permute-start.2 = (f32[1,64,128]{2,1,0:T(8,128)S(1)}, f32[1,64,128]{2,1,0:T(8,128)S(1)}, u32[]{:S(2)}, u32[]{:S(2)}) collective-permute-start(f32[1,64,128]{2,1,0:T(8,128)S(1)} %bitcast.14), channel_id=1, source_target_pairs={{0,3},{1,2},{2,1},{3,0},{4,7},{5,6},{6,5},{7,4},{8,11},{9,10},{10,... | collective-permute-start | bytes 98312 | tf_op jit(solution)/shard_map/ppermute | solution.py:382
  18.7 0.4 collective-permute-start
  19.1 17.9 %collective-permute-done.2 = f32[1,64,128]{2,1,0:T(8,128)S(1)} collective-permute-done((f32[1,64,128]{2,1,0:T(8,128)S(1)}, f32[1,64,128]{2,1,0:T(8,128)S(1)}, u32[]{:S(2)}, u32[]{:S(2)}) %collective-permute-start.2) | collective-permute-done | bytes 32800 | tf_op jit(solution)/shard_map/ppermute | solution.py:382
  37.0 6.5 %collective-permute-done.1 = f32[1,64,128]{2,1,0:T(8,128)S(1)} collective-permute-done((f32[1,64,128]{2,1,0:T(8,128)S(1)}, f32[1,64,128]{2,1,0:T(8,128)S(1)}, u32[]{:S(2)}, u32[]{:S(2)}) %collective-permute-start.1) | collective-permute-done | bytes 32800 | tf_op jit(solution)/shard_map/ppermute | solution.py:382
  43.4 0.0 collective-permute-done
  43.4 2.2 %collective-permute-start.6 = (f32[4,64,128]{2,1,0:T(8,128)S(1)}, f32[4,64,128]{2,1,0:T(8,128)S(1)}, u32[]{:S(2)}, u32[]{:S(2)}) collective-permute-start(f32[4,64,128]{2,1,0:T(8,128)S(1)} %pad_maximum_fusion.refs_0_), channel_id=1, source_target_pairs={{0,24},{1,25},{2,26},{3,27},{4,28},{5,29},{6,30},{7,31},{8,16},{9,... | collective-permute-start | bytes 393224 | tf_op jit(solution)/shard_map/ppermute | solution.py:382
  45.6 0.2 collective-permute-start.5
  45.9 0.3 collective-permute-start.4
  46.2 2.1 %collective-permute-start.3 = (f32[4,64,128]{2,1,0:T(8,128)S(1)}, f32[4,64,128]{2,1,0:T(8,128)S(1)}, u32[]{:S(2)}, u32[]{:S(2)}) collective-permute-start(f32[4,64,128]{2,1,0:T(8,128)S(1)} %pad_maximum_fusion.refs_0_), channel_id=1, source_target_pairs={{0,4},{1,5},{2,6},{3,7},{4,0},{5,1},{6,2},{7,3},{8,12},{9,13},{10,... | collective-permute-start | bytes 393224 | tf_op jit(solution)/shard_map/ppermute | solution.py:382
  48.3 0.0 collective-permute-done.6.refs_4_
  48.3 3.1 %collective-permute-start.9 = (f32[4,64,128]{2,1,0:T(8,128)S(1)}, f32[4,64,128]{2,1,0:T(8,128)S(1)}, u32[]{:S(2)}, u32[]{:S(2)}) collective-permute-start(f32[4,64,128]{2,1,0:T(8,128)S(1)} %collective-permute-done.6.refs_4_), channel_id=1, source_target_pairs={{0,4},{1,5},{2,6},{3,7},{4,0},{5,1},{6,2},{7,3},{8,12},{9,13},{10,... | collective-permute-start | bytes 393224 | tf_op jit(solution)/shard_map/ppermute | solution.py:382
  51.4 0.6 collective-permute-done.5.refs_3_
  52.0 1.1 collective-permute-start.8
  53.1 0.1 collective-permute-start.7
  53.2 1.3 %prepare.1 = (bf16[4,1024,128]{2,1,0:T(8,128)(2,1)S(1)}, f32[4,128]{1,0:T(4,128)S(1)}) custom-call(s32[1]{0:T(128)S(6)} %mul.7.zone_ref, s32[128,128]{1,0:T(8,128)} %neighbours_ref.1, f32[1,1024]{1,0:T(1,128)} %bitcast.20, s32[1,1024]{1,0:T(1,128)} %bitcast.19), custom_call_target="tpu_custom_call" | custom-call | tf_op jit(solution)/shard_map/prepare/pallas_call | solution.py:386
  54.5 10.6 %solve.1.transform_ref = f32[4,128,128]{2,1,0:T(8,128)S(1)} custom-call(s32[1]{0:T(128)} %bitcast.me_ref, bf16[4,1024,128]{2,1,0:T(8,128)(2,1)S(1)} %get-tuple-element.9.pick_ref, f32[4,128]{1,0:T(4,128)S(1)} %get-tuple-element.10.errors_ref, f32[1,1024]{1,0:T(1,128)} %bitcast.22, f32[1,1024]{1,0:T(1,128)} %bitcast.21, ...), custom_call_target="tpu_custom_call" | custom-call | tf_op jit(solution)/shard_map/solve/pallas_call | solution.py:430
  65.2 2.9 %analyse.1 = f32[32,128,128]{2,1,0:T(8,128)} custom-call(s32[32]{0:T(128)} %counts_ref.1, f32[4,128,128]{2,1,0:T(8,128)S(1)} %solve.1.transform_ref, f32[32,64,128]{2,1,0:T(8,128)S(1)} %all-to-all-done.cells_ref), custom_call_target="tpu_custom_call" | custom-call | tf_op jit(solution)/shard_map/analyse/pallas_call | solution.py:443
  68.0 0.0 copy-start.1
  68.0 3.4 %all-to-all-start.1 = ((f32[32,128,128]{2,1,0:T(8,128)}), f32[32,128,128]{2,1,0:T(8,128)S(1)}, u32[]{:S(2)}, u32[]{:S(2)}) async-start(f32[32,128,128]{2,1,0:T(8,128)} %analyse.1), calls=%async_computation.1 | async-start | bytes 4194304 | tf_op jit(solution)/shard_map/all_to_all | solution.py:456
  71.5 0.6 dynamic_slice.3.count_ref
  72.0 47.7 %all-to-all-done.1.rows_ref = f32[32,128,128]{2,1,0:T(8,128)S(1)} async-done(((f32[32,128,128]{2,1,0:T(8,128)}), f32[32,128,128]{2,1,0:T(8,128)S(1)}, u32[]{:S(2)}, u32[]{:S(2)}) %all-to-all-start.1) | async-done | bytes 2097184 | tf_op jit(solution)/shard_map/all_to_all | solution.py:456
  119.8 3.3 %advance.1 = f32[8,65536]{1,0:T(8,128)} custom-call(s32[1]{0:T(128)} %dynamic_slice.3.count_ref, f32[32,128,128]{2,1,0:T(8,128)S(1)} %all-to-all-done.1.rows_ref), custom_call_target="tpu_custom_call" | custom-call | tf_op jit(solution)/shard_map/advance/pallas_call | solution.py:459
  (11 shorter events, 0.0 us)
Async XLA Ops:
  8.3 7.1 %copy-start = (f32[64,128]{1,0:T(8,128)S(1)}, f32[64,128]{1,0:T(8,128)}, u32[]{:S(2)}) copy-start(f32[64,128]{1,0:T(8,128)} %get-tuple-element.11) | copy-start | bytes 98308
  8.3 56.8 %all-to-all-start = ((f32[32,64,128]{2,1,0:T(8,128)}), f32[32,64,128]{2,1,0:T(8,128)S(1)}, u32[]{:S(2)}, u32[]{:S(2)}) async-start(f32[32,64,128]{2,1,0:T(8,128)} %bitcast.13), calls=%async_computation | async-start | bytes 2097152 | tf_op jit(solution)/shard_map/all_to_all | solution.py:423
  15.4 21.5 %collective-permute-start.2 = (f32[1,64,128]{2,1,0:T(8,128)S(1)}, f32[1,64,128]{2,1,0:T(8,128)S(1)}, u32[]{:S(2)}, u32[]{:S(2)}) collective-permute-start(f32[1,64,128]{2,1,0:T(8,128)S(1)} %bitcast.14), channel_id=1, source_target_pairs={{0,3},{1,2},{2,1},{3,0},{4,7},{5,6},{6,5},{7,4},{8,11},{9,10},{10,... | collective-permute-start | bytes 98312 | tf_op jit(solution)/shard_map/ppermute | solution.py:382
  18.7 24.7 %collective-permute-start.1 = (f32[1,64,128]{2,1,0:T(8,128)S(1)}, f32[1,64,128]{2,1,0:T(8,128)S(1)}, u32[]{:S(2)}, u32[]{:S(2)}) collective-permute-start(f32[1,64,128]{2,1,0:T(8,128)S(1)} %bitcast.15), channel_id=1, source_target_pairs={{0,2},{1,3},{2,0},{3,1},{4,6},{5,7},{6,4},{7,5},{8,10},{9,11},{10,... | collective-permute-start | bytes 98312 | tf_op jit(solution)/shard_map/ppermute | solution.py:382
  18.7 24.7 %collective-permute-start = (f32[1,64,128]{2,1,0:T(8,128)S(1)}, f32[1,64,128]{2,1,0:T(8,128)S(1)}, u32[]{:S(2)}, u32[]{:S(2)}) collective-permute-start(f32[1,64,128]{2,1,0:T(8,128)S(1)} %bitcast.16), channel_id=1, source_target_pairs={{0,1},{1,0},{2,3},{3,2},{4,5},{5,4},{6,7},{7,6},{8,9},{9,8},{10,11... | collective-permute-start | bytes 98312 | tf_op jit(solution)/shard_map/ppermute | solution.py:382
  43.4 4.8 %collective-permute-start.6 = (f32[4,64,128]{2,1,0:T(8,128)S(1)}, f32[4,64,128]{2,1,0:T(8,128)S(1)}, u32[]{:S(2)}, u32[]{:S(2)}) collective-permute-start(f32[4,64,128]{2,1,0:T(8,128)S(1)} %pad_maximum_fusion.refs_0_), channel_id=1, source_target_pairs={{0,24},{1,25},{2,26},{3,27},{4,28},{5,29},{6,30},{7,31},{8,16},{9,... | collective-permute-start | bytes 393224 | tf_op jit(solution)/shard_map/ppermute | solution.py:382
  45.6 6.4 %collective-permute-start.5 = (f32[4,64,128]{2,1,0:T(8,128)S(1)}, f32[4,64,128]{2,1,0:T(8,128)S(1)}, u32[]{:S(2)}, u32[]{:S(2)}) collective-permute-start(f32[4,64,128]{2,1,0:T(8,128)S(1)} %pad_maximum_fusion.refs_0_), channel_id=1, source_target_pairs={{0,16},{1,17},{2,18},{3,19},{4,20},{5,21},{6,22},{7,23},{8,24},{9,... | collective-permute-start | bytes 393224 | tf_op jit(solution)/shard_map/ppermute | solution.py:382
  45.9 7.3 %collective-permute-start.4 = (f32[4,64,128]{2,1,0:T(8,128)S(1)}, f32[4,64,128]{2,1,0:T(8,128)S(1)}, u32[]{:S(2)}, u32[]{:S(2)}) collective-permute-start(f32[4,64,128]{2,1,0:T(8,128)S(1)} %pad_maximum_fusion.refs_0_), channel_id=1, source_target_pairs={{0,8},{1,9},{2,10},{3,11},{4,12},{5,13},{6,14},{7,15},{8,0},{9,1},... | collective-permute-start | bytes 393224 | tf_op jit(solution)/shard_map/ppermute | solution.py:382
  46.2 8.3 %collective-permute-start.3 = (f32[4,64,128]{2,1,0:T(8,128)S(1)}, f32[4,64,128]{2,1,0:T(8,128)S(1)}, u32[]{:S(2)}, u32[]{:S(2)}) collective-permute-start(f32[4,64,128]{2,1,0:T(8,128)S(1)} %pad_maximum_fusion.refs_0_), channel_id=1, source_target_pairs={{0,4},{1,5},{2,6},{3,7},{4,0},{5,1},{6,2},{7,3},{8,12},{9,13},{10,... | collective-permute-start | bytes 393224 | tf_op jit(solution)/shard_map/ppermute | solution.py:382
  48.3 6.2 %collective-permute-start.9 = (f32[4,64,128]{2,1,0:T(8,128)S(1)}, f32[4,64,128]{2,1,0:T(8,128)S(1)}, u32[]{:S(2)}, u32[]{:S(2)}) collective-permute-start(f32[4,64,128]{2,1,0:T(8,128)S(1)} %collective-permute-done.6.refs_4_), channel_id=1, source_target_pairs={{0,4},{1,5},{2,6},{3,7},{4,0},{5,1},{6,2},{7,3},{8,12},{9,13},{10,... | collective-permute-start | bytes 393224 | tf_op jit(solution)/shard_map/ppermute | solution.py:382
  52.0 2.5 %collective-permute-start.8 = (f32[4,64,128]{2,1,0:T(8,128)S(1)}, f32[4,64,128]{2,1,0:T(8,128)S(1)}, u32[]{:S(2)}, u32[]{:S(2)}) collective-permute-start(f32[4,64,128]{2,1,0:T(8,128)S(1)} %collective-permute-done.5.refs_3_), channel_id=1, source_target_pairs={{0,4},{1,5},{2,6},{3,7},{4,0},{5,1},{6,2},{7,3},{8,12},{9,13},{10,... | collective-permute-start | bytes 393224 | tf_op jit(solution)/shard_map/ppermute | solution.py:382
  53.1 1.4 %collective-permute-start.7 = (f32[4,64,128]{2,1,0:T(8,128)S(1)}, f32[4,64,128]{2,1,0:T(8,128)S(1)}, u32[]{:S(2)}, u32[]{:S(2)}) collective-permute-start(f32[4,64,128]{2,1,0:T(8,128)S(1)} %collective-permute-done.4.refs_2_), channel_id=1, source_target_pairs={{0,4},{1,5},{2,6},{3,7},{4,0},{5,1},{6,2},{7,3},{8,12},{9,13},{10,... | collective-permute-start | bytes 393224 | tf_op jit(solution)/shard_map/ppermute | solution.py:382
  68.0 3.4 %copy-start.1 = (s32[32]{0:T(128)S(1)}, s32[32]{0:T(128)}, u32[]{:S(2)}) copy-start(s32[32]{0:T(128)} %counts_ref.1) | copy-start | bytes 388
  68.0 51.7 %all-to-all-start.1 = ((f32[32,128,128]{2,1,0:T(8,128)}), f32[32,128,128]{2,1,0:T(8,128)S(1)}, u32[]{:S(2)}, u32[]{:S(2)}) async-start(f32[32,128,128]{2,1,0:T(8,128)} %analyse.1), calls=%async_computation.1 | async-start | bytes 4194304 | tf_op jit(solution)/shard_map/all_to_all | solution.py:456
